TPU v7x, 32 devices: a whole 2x2x4 slice. The times are simulated.
32 devices in a mesh: dp: 2 (over x), ep: 16 (over z, y, core).
Axes of the slice: x: 2, y: 2, z: 4, core: 2. Of those that a mesh axis runs over, the one named last changes fastest.
Arguments:
- hidden_in: bfloat16 [1024, 2048], P(('dp', 'ep')), parts along dimension 0
- kv_cache: bfloat16 [1024, 256, 576], P(('dp', 'ep')), parts along dimension 0
- kv_lens: int32 [1024], P(('dp', 'ep')), parts along dimension 0
- routes: int32 [1024, 6], P(('dp', 'ep')), parts along dimension 0
- route_gates: float32 [1024, 6], P(('dp', 'ep')), parts along dimension 0
- w_q: bfloat16 [2048, 3072], replicated
- w_dkv: bfloat16 [2048, 576], replicated
- w_uk: bfloat16 [16, 128, 512], replicated
- w_uv: bfloat16 [16, 512, 128], replicated
- w_o: bfloat16 [2048, 2048], replicated
- sh_gate: bfloat16 [2048, 2816], replicated
- sh_up: bfloat16 [2048, 2816], replicated
- sh_down: bfloat16 [2816, 2048], replicated
- ex_gate: bfloat16 [64, 2048, 1408], P('ep')
- ex_up: bfloat16 [64, 2048, 1408], P('ep')
- ex_down: bfloat16 [64, 1408, 2048], P('ep')
Outputs:
- output 1: bfloat16 [1024, 2048], P(('dp', 'ep')), parts along dimension 0
- output 2: bfloat16 [1024, 576], P(('dp', 'ep')), parts along dimension 0
There are 2 independent parts. A program takes and returns all parts, laid end to end along the dimension named above; an argument that names none is the same for every part.
All inputs are finite; a program needn't handle non-finite values.
Results may differ from a plain program's by a relative error of at most 0.0158526.
Values are sent between devices in bfloat16 or wider.
A program may use at most 1 GiB of HBM per device.

v0:
```python
import jax
import jax.numpy as jnp
from jax import lax
from jax.sharding import PartitionSpec as P


def rotary(vec, cos_t, sin_t):
    half_dim = vec.shape[-1] // 2
    lead_part = vec[..., :half_dim]
    tail_part = vec[..., half_dim:]
    return jnp.concatenate([lead_part * cos_t - tail_part * sin_t, tail_part * cos_t + lead_part * sin_t], axis=-1)


def rotary_table(positions, rot_width):
    half_dim = rot_width // 2
    inv_freq = jnp.exp(jnp.arange(half_dim, dtype=jnp.float32) * (-2.0 * jnp.log(10000.0) / rot_width))
    angle_val = positions.astype(jnp.float32)[:, None] * inv_freq[None, :]
    return jnp.cos(angle_val), jnp.sin(angle_val)


def attend_local(x_blk, cache_blk, len_blk, w_q, w_dkv, w_uk, w_uv, w_o):
    num_seq = x_blk.shape[0]
    num_heads, nope_dim, latent = w_uk.shape
    rope_dim = cache_blk.shape[2] - latent
    v_dim = w_uv.shape[2]
    q_all = jnp.dot(x_blk, w_q, preferred_element_type=jnp.float32).astype(jnp.bfloat16).reshape(num_seq, num_heads, nope_dim + rope_dim)
    kv_raw = jnp.dot(x_blk, w_dkv, preferred_element_type=jnp.float32)
    cos_t, sin_t = rotary_table(len_blk, rope_dim)
    kv_row = jnp.concatenate([kv_raw[:, :latent], rotary(kv_raw[:, latent:], cos_t, sin_t)], axis=1).astype(jnp.bfloat16)
    q_rope = rotary(q_all[:, :, nope_dim:].astype(jnp.float32), cos_t[:, None, :], sin_t[:, None, :]).astype(jnp.bfloat16)
    q_lat = jnp.einsum("bhn,hnc->bhc", q_all[:, :, :nope_dim], w_uk, preferred_element_type=jnp.float32).astype(jnp.bfloat16)
    q_cat = jnp.concatenate([q_lat, q_rope], axis=2)
    score_scale = (nope_dim + rope_dim) ** -0.5
    s_old = jnp.einsum("bhc,blc->bhl", q_cat, cache_blk, preferred_element_type=jnp.float32) * score_scale
    s_new = jnp.einsum("bhc,bc->bh", q_cat, kv_row, preferred_element_type=jnp.float32) * score_scale
    valid_mask = jnp.arange(cache_blk.shape[1])[None, None, :] < len_blk[:, None, None]
    s_old = jnp.where(valid_mask, s_old, -jnp.inf)
    top_score = jnp.maximum(jnp.max(s_old, axis=2), s_new)
    e_old = jnp.exp(s_old - top_score[:, :, None])
    e_new = jnp.exp(s_new - top_score)
    denom_sum = jnp.sum(e_old, axis=2) + e_new
    p_old = (e_old / denom_sum[:, :, None]).astype(jnp.bfloat16)
    p_new = (e_new / denom_sum).astype(jnp.bfloat16)
    o_full = jnp.einsum("bhl,blc->bhc", p_old, cache_blk, preferred_element_type=jnp.float32) + p_new.astype(jnp.float32)[:, :, None] * kv_row.astype(jnp.float32)[:, None, :]
    o_lat = o_full[:, :, :latent].astype(jnp.bfloat16)
    v_head = jnp.einsum("bhc,hcv->bhv", o_lat, w_uv, preferred_element_type=jnp.float32).astype(jnp.bfloat16)
    attn_out = jnp.dot(v_head.reshape(num_seq, num_heads * v_dim), w_o, preferred_element_type=jnp.float32).astype(jnp.bfloat16)
    h_mid = (x_blk.astype(jnp.float32) + attn_out.astype(jnp.float32)).astype(jnp.bfloat16)
    return h_mid, kv_row


def swiglu(rows_in, w_gate, w_up, w_down):
    gate_val = jnp.dot(rows_in, w_gate, preferred_element_type=jnp.float32)
    up_val = jnp.dot(rows_in, w_up, preferred_element_type=jnp.float32)
    act_val = (jax.nn.silu(gate_val) * up_val).astype(jnp.bfloat16)
    return jnp.dot(act_val, w_down, preferred_element_type=jnp.float32).astype(jnp.bfloat16)


def expert_rows(row_buf, ex_gate, ex_up, ex_down):
    gate_val = jnp.einsum("gch,ghf->gcf", row_buf, ex_gate, preferred_element_type=jnp.float32)
    up_val = jnp.einsum("gch,ghf->gcf", row_buf, ex_up, preferred_element_type=jnp.float32)
    act_val = (jax.nn.silu(gate_val) * up_val).astype(jnp.bfloat16)
    return jnp.einsum("gcf,gfh->gch", act_val, ex_down, preferred_element_type=jnp.float32).astype(jnp.bfloat16)


def expert_cap(seqs_dev, top_k, group_size, local_exp):
    hot_devs = group_size // 4
    pair_cap = (seqs_dev * ((3 * top_k) // 4) + hot_devs - 1) // hot_devs
    return (pair_cap + local_exp - 1) // local_exp


def solution(mesh):
    group_size = mesh.shape["ep"]

    def device_step(x_blk, cache_blk, len_blk, routes, route_gates, w_q, w_dkv, w_uk, w_uv, w_o, sh_gate, sh_up, sh_down, ex_gate, ex_up, ex_down):
        num_seq, hidden = x_blk.shape
        top_k = routes.shape[1]
        local_exp = ex_gate.shape[0]
        num_exp = local_exp * group_size
        exp_cap = expert_cap(num_seq, top_k, group_size, local_exp)
        h_mid, kv_row = attend_local(x_blk, cache_blk, len_blk, w_q, w_dkv, w_uk, w_uv, w_o)
        shared = swiglu(h_mid, sh_gate, sh_up, sh_down)
        flat_ids = routes.reshape(-1)
        onehot = (flat_ids[:, None] == jnp.arange(num_exp, dtype=jnp.int32)[None, :]).astype(jnp.int32)
        rank_pos = jnp.sum((jnp.cumsum(onehot, axis=0) - onehot) * onehot, axis=1)
        slot_idx = (flat_ids % local_exp) * (group_size * exp_cap) + (flat_ids // local_exp) * exp_cap + rank_pos
        token_ids = jnp.arange(num_seq * top_k, dtype=jnp.int32) // top_k
        slot_token = jnp.zeros((num_exp * exp_cap,), jnp.int32).at[slot_idx].set(token_ids)
        send_buf = jnp.take(h_mid, slot_token, axis=0).reshape(local_exp, group_size, exp_cap, hidden)
        recv_buf = lax.all_to_all(send_buf, "ep", 1, 1, tiled=True)
        exp_out = expert_rows(recv_buf.reshape(local_exp, group_size * exp_cap, hidden), ex_gate, ex_up, ex_down)
        back_buf = lax.all_to_all(exp_out.reshape(local_exp, group_size, exp_cap, hidden), "ep", 1, 1, tiled=True)
        picked = jnp.take(back_buf.reshape(num_exp * exp_cap, hidden), slot_idx, axis=0).reshape(num_seq, top_k, hidden)
        routed = jnp.sum(picked.astype(jnp.float32) * route_gates[:, :, None], axis=1)
        layer_out = (h_mid.astype(jnp.float32) + shared.astype(jnp.float32) + routed).astype(jnp.bfloat16)
        return layer_out, kv_row

    batch_spec = P(("dp", "ep"))
    weight_spec = P()
    expert_spec = P("ep")
    in_specs = (batch_spec,) * 5 + (weight_spec,) * 8 + (expert_spec,) * 3
    return jax.shard_map(device_step, mesh=mesh, in_specs=in_specs, out_specs=(batch_spec, batch_spec), check_vma=False)
```

profile of v0, /device:TPU:15, one launch (start us, length us, event | category | flops | bytes accessed | tf_op | source)
XLA Modules:
  0.0 190.6 jit_solution(7708317461430422179)
XLA Ops:
  0.7 7.0 %convolution_convert_fusion = bf16[32,3072]{1,0:T(8,128)(2,1)S(1)} fusion(bf16[32,2048]{1,0:T(8,128)(2,1)} %param.16, bf16[2048,3072]{1,0:T(8,128)(2,1)} %param.21), kind=kOutput, calls=%fused_computation.6 | convolution fusion | flops 402751488 | bytes 12910592 | tf_op jit(solution)/shard_map/dot_general | solution.py:26
  7.8 0.3 reshape.280
  8.2 0.8 fusion.56
  9.7 0.6 reduce-window.6
  10.7 1.2 scatter_custom_fusion
  12.0 2.0 %fusion.15 = bf16[32,16,512]{2,0,1:T(8,128)(2,1)S(1)} fusion(bf16[16,128,512]{2,1,0:T(8,128)(2,1)} %param.23, bf16[32,16,128]{2,1,0:T(8,128)(2,1)S(1)} %slice.53), kind=kOutput, calls=%fused_computation.27 | convolution fusion | flops 67371008 | bytes 2752512 | tf_op jit(solution)/shard_map/bhn,hnc->bhc/dot_general | solution.py:31
  14.3 0.4 fusion.19
  14.6 5.4 %fusion.55 = (f32[32,16]{1,0:T(8,128)S(1)}, f32[32,16,256]{2,1,0:T(8,128)S(1)}) fusion(bf16[32,256,576]{1,2,0:T(8,128)(2,1)} %param.17, bf16[32,16,576]{2,0,1:T(8,128)(2,1)S(1)} %pad_maximum_fusion, pred[32,256]{1,0:T(8,128)(4,1)S(1)} %iota_compare_fusion.2), kind=kOutput, calls=%fused_computation.117 | convolution fusion | flops 151387648 | bytes 10561536 | tf_op jit(solution)/shard_map/bhc,blc->bhl/dot_general | solution.py:34
  20.7 2.6 %fusion.29 = f32[32,16,576]{2,1,0:T(8,128)S(1)} fusion(bf16[32,256,576]{1,2,0:T(8,128)(2,1)S(1)} %bitcast.54, f32[32,16,256]{2,1,0:T(8,128)S(1)} %get-tuple-element.11, f32[32,16]{1,0:T(8,128)S(1)} %get-tuple-element.7, f32[32,16]{1,0:T(8,128)S(1)} %multiply_maximum_fusion), kind=kOutput, calls=%fused_computation.47 | convolution fusion | flops 151388160 | bytes 11145216 | tf_op jit(solution)/shard_map/bhl,blc->bhc/dot_general | solution.py:44
  23.6 2.2 %fusion.17 = bf16[16,4,8,128]{3,2,1,0:T(8,128)(2,1)S(1)} fusion(bf16[16,512,128]{2,1,0:T(8,128)(2,1)} %param.24, bf16[32,16,512]{2,1,0:T(8,128)(2,1)S(1)} %fusion.18), kind=kOutput, calls=%fused_computation.31 | convolution fusion | flops 67174400 | bytes 2752512 | tf_op jit(solution)/shard_map/bhc,hcv->bhv/dot_general | solution.py:46
  25.8 4.9 %fusion.9 = bf16[32,2048]{1,0:T(8,128)(2,1)S(1)} fusion(bf16[2048,2048]{1,0:T(8,128)(2,1)} %param.25, bf16[32,2048]{1,0:T(8,128)(2,1)S(1)} %copy-done.2, bf16[16,4,8,128]{3,2,1,0:T(8,128)(2,1)S(1)} %fusion.17), kind=kOutput, calls=%fused_computation.18 | convolution fusion | flops 268763136 | bytes 8781824 | tf_op jit(solution)/shard_map/dot_general | solution.py:47
  30.7 2.5 %gather_fusion = bf16[512,2048]{1,0:T(8,128)(2,1)S(1)} fusion(bf16[32,2048]{1,0:T(8,128)(2,1)S(1)} %fusion.9, s32[1024]{0:T(1024)S(1)} %pad_clamp_fusion.1), kind=kCustom, calls=%fused_computation | custom fusion | bytes 4196352 | tf_op jit(solution)/shard_map/jit(_take)/gather | solution.py:89
  33.5 54.0 %all_to_all.10 = bf16[4,16,8,2048]{3,2,0,1:T(8,128)(2,1)S(1)} all-to-all(bf16[4,16,8,2048]{3,2,0,1:T(8,128)(2,1)S(1)} %copy_select_fusion), channel_id=1, replica_groups=mesh['dp'=2,'ep'=16] {'ep'}, dimensions={1} | all-to-all | bytes 4194304 | tf_op jit(solution)/shard_map/all_to_all | solution.py:90
  87.5 9.4 %fusion.11 = f32[4,128,1408]{2,1,0:T(8,128)S(1)} fusion(bf16[4,2048,1408]{2,1,0:T(8,128)(2,1)} %param.29, bf16[4,16,8,2048]{3,2,0,1:T(8,128)(2,1)S(1)} %all_to_all.10), kind=kOutput, calls=%fused_computation.20 | convolution fusion | flops 2952790016 | bytes 28049408 | tf_op jit(solution)/shard_map/gch,ghf->gcf/dot_general | solution.py:60
  96.9 11.4 %fusion.1 = bf16[4,128,1408]{2,1,0:T(8,128)(2,1)S(1)} fusion(bf16[4,2048,1408]{2,1,0:T(8,128)(2,1)} %param.30, f32[4,128,1408]{2,1,0:T(8,128)S(1)} %fusion.11, bf16[4,16,8,2048]{3,2,0,1:T(8,128)(2,1)S(1)} %all_to_all.10), kind=kOutput, calls=%fused_computation.8 | convolution fusion | flops 2957115392 | bytes 29491200 | tf_op jit(solution)/shard_map/gch,ghf->gcf/dot_general | solution.py:61
  108.3 11.0 %fusion.2 = bf16[4,16,8,2048]{3,2,1,0:T(8,128)(2,1)S(1)} fusion(bf16[4,128,1408]{2,1,0:T(8,128)(2,1)S(1)} %fusion.1, bf16[4,1408,2048]{2,1,0:T(8,128)(2,1)} %param.31), kind=kOutput, calls=%fused_computation.9 | convolution fusion | flops 2953838592 | bytes 26607616 | tf_op jit(solution)/shard_map/gcf,gfh->gch/dot_general | solution.py:63
  119.3 1.5 copy.54
  120.9 4.7 %all-to-all-start.1 = ((bf16[4,16,8,2048]{3,2,0,1:T(8,128)(2,1)}), bf16[4,16,8,2048]{3,2,0,1:T(8,128)(2,1)}, u32[]{:S(2)}, u32[]{:S(2)}) async-start(bf16[4,16,8,2048]{3,2,0,1:T(8,128)(2,1)} %copy.54), calls=%async_computation.1 | async-start | bytes 4194304 | tf_op jit(solution)/shard_map/all_to_all | solution.py:92
  125.8 7.1 %fusion.57 = f32[32,2816]{1,0:T(8,128)} fusion(bf16[32,2048]{1,0:T(8,128)(2,1)S(1)} %fusion.9, bf16[2048,2816]{1,0:T(8,128)(2,1)} %param.26), kind=kOutput, calls=%fused_computation.119 | convolution fusion | flops 369098752 | bytes 12025856 | tf_op jit(solution)/shard_map/dot_general | solution.py:53
  132.9 40.3 %all-to-all-done.1 = bf16[4,16,8,2048]{3,2,0,1:T(8,128)(2,1)} async-done(((bf16[4,16,8,2048]{3,2,0,1:T(8,128)(2,1)}), bf16[4,16,8,2048]{3,2,0,1:T(8,128)(2,1)}, u32[]{:S(2)}, u32[]{:S(2)}) %all-to-all-start.1) | async-done | bytes 2097184 | tf_op jit(solution)/shard_map/all_to_all | solution.py:92
  173.2 1.8 copy.55
  175.1 1.2 gather_fusion.1
  176.5 1.6 multiply_reduce_fusion
  178.1 12.5 %fusion.6 = bf16[32,2048]{1,0:T(8,128)(2,1)} fusion(f32[32,2048]{1,0:T(8,128)S(1)} %multiply_reduce_fusion, bf16[2816,2048]{1,0:T(8,128)(2,1)} %param.28, bf16[32,2048]{1,0:T(8,128)(2,1)S(1)} %fusion.9, bf16[2048,2816]{1,0:T(8,128)(2,1)} %param.27, f32[32,2816]{1,0:T(8,128)} %fusion.57), kind=kOutput, calls=%fused_computation.14 | convolution fusion | flops 739131392 | bytes 23953408 | tf_op jit(solution)/shard_map/dot_general | solution.py:56
  (61 shorter events, 3.2 us)
Async XLA Ops:
  0.6 7.6 %copy-start = (bf16[2048,576]{0,1:T(8,128)(2,1)S(1)}, bf16[2048,576]{0,1:T(8,128)(2,1)}, u32[]{:S(2)}) copy-start(bf16[2048,576]{0,1:T(8,128)(2,1)} %param.22) | copy-start | bytes 7077892
  0.7 7.5 %copy-start.6 = (s32[32]{0:T(128)S(1)}, s32[32]{0:T(128)}, u32[]{:S(2)}) copy-start(s32[32]{0:T(128)} %param.18) | copy-start | bytes 388
  0.7 7.6 %copy-start.2 = (bf16[32,2048]{1,0:T(8,128)(2,1)S(1)}, bf16[32,2048]{1,0:T(8,128)(2,1)}, u32[]{:S(2)}) copy-start(bf16[32,2048]{1,0:T(8,128)(2,1)} %param.16) | copy-start | bytes 393220
  7.7 1.6 copy-start.4
  9.3 13.9 %copy-start.3 = (bf16[32,576]{1,0:T(8,128)(2,1)}, bf16[32,576]{1,0:T(8,128)(2,1)S(1)}, u32[]{:S(2)}) copy-start(bf16[32,576]{1,0:T(8,128)(2,1)S(1)} %pad_maximum_fusion.1) | copy-start | bytes 110596
  14.3 6.1 %slice-start = ((s8[9437184]{0:T(1024)(128)(4,1)}), s8[4194304]{0:T(1024)(128)(4,1)S(1)}, s32[]{:S(2)}) async-start(s8[9437184]{0:T(1024)(128)(4,1)} %bitcast.53), calls=%async_computation.2 | async-start | bytes 8388608
  14.6 5.9 %slice-start.1 = ((s8[9437184]{0:T(1024)(128)(4,1)}), s8[4194304]{0:T(1024)(128)(4,1)S(1)}, s32[]{:S(2)}) async-start(s8[9437184]{0:T(1024)(128)(4,1)} %bitcast.53), calls=%async_computation.3 | async-start | bytes 8388608
  14.6 6.1 %slice-start.2 = ((s8[9437184]{0:T(1024)(128)(4,1)}), s8[1048576]{0:T(1024)(128)(4,1)S(1)}, s32[]{:S(2)}) async-start(s8[9437184]{0:T(1024)(128)(4,1)} %bitcast.53), calls=%async_computation.4 | async-start | bytes 2097152
  120.9 4.8 %copy-start.5 = (f32[32,6]{0,1:T(8,128)S(1)}, f32[32,6]{0,1:T(8,128)}, u32[]{:S(2)}) copy-start(f32[32,6]{0,1:T(8,128)} %param.20) | copy-start | bytes 2308
  120.9 52.4 %all-to-all-start.1 = ((bf16[4,16,8,2048]{3,2,0,1:T(8,128)(2,1)}), bf16[4,16,8,2048]{3,2,0,1:T(8,128)(2,1)}, u32[]{:S(2)}, u32[]{:S(2)}) async-start(bf16[4,16,8,2048]{3,2,0,1:T(8,128)(2,1)} %copy.54), calls=%async_computation.1 | async-start | bytes 4194304 | tf_op jit(solution)/shard_map/all_to_all | solution.py:92
  178.1 12.5 %copy-start.1 = (bf16[2048,576]{0,1:T(8,128)(2,1)S(1)}, bf16[2048,576]{0,1:T(8,128)(2,1)}, u32[]{:S(2)}) copy-start(bf16[2048,576]{0,1:T(8,128)(2,1)} %param.22) | copy-start | bytes 7077892
where the time goes:
time: 191 us
  matrix products  76.7 us (40%)
  blocking collectives  54 us (28%)
  waiting for transfers between devices  40.3 us (21%)
  local copies, waits for them, and re-layouts  10 us (5%)
  starting transfers between devices  4.7 us (2%)
  other arithmetic  3.85 us (2%)
    all_to_all x1, blocking collectives, device_step(): recv_buf = lax.all_to_all(send_buf, 'ep', 1, 1, tiled=True)  54 us
    all_to_all x1, waiting for transfers between devices, device_step(): lax.all_to_all(exp_out.reshape(local_exp, group_size, exp_cap, hidden), '...  40.3 us
    dot_general x1, matrix products, swiglu(): jnp.dot(act_val, w_down, preferred_element_type=jnp.float32)  12.5 us
    dot_general x1, matrix products, expert_rows(): jnp.einsum('gch,ghf->gcf', row_buf, ex_up, preferred_element_type=jnp.flo...  11.4 us
    dot_general x1, matrix products, expert_rows(): jnp.einsum('gcf,gfh->gch', act_val, ex_down, preferred_element_type=jnp.f...  11 us
    dot_general x1, matrix products, expert_rows(): jnp.einsum('gch,ghf->gcf', row_buf, ex_gate, preferred_element_type=jnp.f...  9.39 us
    dot_general x1, matrix products, swiglu(): gate_val = jnp.dot(rows_in, w_gate, preferred_element_type=jnp.float32)  7.07 us
    dot_general x1, matrix products, attend_local(): jnp.dot(x_blk, w_q, preferred_element_type=jnp.float32).astype(jnp.bfloat16)  7.05 us
  transfers between devices with their start and end apart: 1, of which 1 were waited for; matrix products, arithmetic and copies ran while one was open for 4% of the time, Pallas kernels for 0%

commit v1 on v0

--- a/solution.py
+++ b/solution.py
@@ -76,22 +76,29 @@
         num_seq, hidden = x_blk.shape
         top_k = routes.shape[1]
         local_exp = ex_gate.shape[0]
-        num_exp = local_exp * group_size
         exp_cap = expert_cap(num_seq, top_k, group_size, local_exp)
         h_mid, kv_row = attend_local(x_blk, cache_blk, len_blk, w_q, w_dkv, w_uk, w_uv, w_o)
         shared = swiglu(h_mid, sh_gate, sh_up, sh_down)
-        flat_ids = routes.reshape(-1)
-        onehot = (flat_ids[:, None] == jnp.arange(num_exp, dtype=jnp.int32)[None, :]).astype(jnp.int32)
-        rank_pos = jnp.sum((jnp.cumsum(onehot, axis=0) - onehot) * onehot, axis=1)
-        slot_idx = (flat_ids % local_exp) * (group_size * exp_cap) + (flat_ids // local_exp) * exp_cap + rank_pos
-        token_ids = jnp.arange(num_seq * top_k, dtype=jnp.int32) // top_k
-        slot_token = jnp.zeros((num_exp * exp_cap,), jnp.int32).at[slot_idx].set(token_ids)
-        send_buf = jnp.take(h_mid, slot_token, axis=0).reshape(local_exp, group_size, exp_cap, hidden)
-        recv_buf = lax.all_to_all(send_buf, "ep", 1, 1, tiled=True)
-        exp_out = expert_rows(recv_buf.reshape(local_exp, group_size * exp_cap, hidden), ex_gate, ex_up, ex_down)
-        back_buf = lax.all_to_all(exp_out.reshape(local_exp, group_size, exp_cap, hidden), "ep", 1, 1, tiled=True)
-        picked = jnp.take(back_buf.reshape(num_exp * exp_cap, hidden), slot_idx, axis=0).reshape(num_seq, top_k, hidden)
-        routed = jnp.sum(picked.astype(jnp.float32) * route_gates[:, :, None], axis=1)
+        me = lax.axis_index("ep")
+        ids_all = lax.all_gather(routes, "ep", tiled=True)
+        gates_all = lax.all_gather(route_gates, "ep", tiled=True)
+        h_all = lax.all_gather(h_mid, "ep", tiled=True)
+        num_tok = num_seq * group_size
+        exp_ids = me * local_exp + jnp.arange(local_exp, dtype=jnp.int32)
+        hit = ids_all[:, :, None] == exp_ids[None, None, :]
+        member = jnp.any(hit, axis=1)
+        gate_te = jnp.sum(jnp.where(hit, gates_all[:, :, None], 0.0), axis=1)
+        tri = (jnp.arange(num_seq)[:, None] > jnp.arange(num_seq)[None, :]).astype(jnp.bfloat16)
+        rank = jnp.einsum("ts,dse->dte", tri, member.astype(jnp.bfloat16).reshape(group_size, num_seq, local_exp), preferred_element_type=jnp.float32)
+        base = (jnp.arange(group_size, dtype=jnp.int32) * exp_cap)[:, None, None]
+        slot = jnp.where(member, (rank.astype(jnp.int32) + base).reshape(num_tok, local_exp), -1)
+        rows_exp = group_size * exp_cap
+        pick = (slot.T[:, None, :] == jnp.arange(rows_exp, dtype=jnp.int32)[None, :, None]).astype(jnp.bfloat16)
+        recv = jnp.einsum("est,th->esh", pick, h_all, preferred_element_type=jnp.float32).astype(jnp.bfloat16)
+        exp_out = expert_rows(recv, ex_gate, ex_up, ex_down)
+        back = jnp.einsum("est,esh->eth", pick, exp_out, preferred_element_type=jnp.float32)
+        part = jnp.sum(back * gate_te.T[:, :, None], axis=0)
+        routed = lax.psum_scatter(part, "ep", scatter_dimension=0, tiled=True)
         layer_out = (h_mid.astype(jnp.float32) + shared.astype(jnp.float32) + routed).astype(jnp.bfloat16)
         return layer_out, kv_row
 

time: 191 us -> 202 us (1.058)
  the two profiles are of different devices: /device:TPU:15 before, /device:TPU:0 now
where the time goes in v1:
time: 202 us
  matrix products  75.2 us (37%)
  waiting for transfers between devices  67.2 us (33%)
  blocking collectives  41.4 us (20%)
  between operations  14.3 us (7%)
  local copies, waits for them, and re-layouts  2.47 us (1%)
    reduce_scatter x1, waiting for transfers between devices, device_step(): routed = lax.psum_scatter(part, 'ep', scatter_dimension=0, tiled=True)  64.5 us
    all_gather x1, blocking collectives, device_step(): gates_all = lax.all_gather(route_gates, 'ep', tiled=True)  23.4 us
    all_gather x1, blocking collectives, device_step(): ids_all = lax.all_gather(routes, 'ep', tiled=True)  18 us
    dot_general x1, matrix products, device_step(): jnp.einsum('est,esh->eth', pick, exp_out, preferred_element_type=jnp.floa...  13.5 us
    dot_general x1, matrix products, expert_rows(): jnp.einsum('gch,ghf->gcf', row_buf, ex_up, preferred_element_type=jnp.flo...  12.6 us
    dot_general x1, matrix products, swiglu(): jnp.dot(act_val, w_down, preferred_element_type=jnp.float32)  12.4 us
    dot_general x1, matrix products, expert_rows(): jnp.einsum('gch,ghf->gcf', row_buf, ex_gate, preferred_element_type=jnp.f...  9.4 us
    dot_general x1, matrix products, attend_local(): jnp.dot(x_blk, w_q, preferred_element_type=jnp.float32).astype(jnp.bfloat16)  7.05 us
  transfers between devices with their start and end apart: 2, of which 2 were waited for; matrix products, arithmetic and copies ran while one was open for 3% of the time, Pallas kernels for 0%

profile of v1, /device:TPU:0, one launch (start us, length us, event | category | flops | bytes accessed | tf_op | source)
XLA Modules:
  0.0 202.0 jit_solution(10210823743998281009)
XLA Ops:
  7.3 7.0 %convolution_convert_fusion = bf16[32,3072]{1,0:T(8,128)(2,1)S(1)} fusion(bf16[32,2048]{1,0:T(8,128)(2,1)} %param.16, bf16[2048,3072]{1,0:T(8,128)(2,1)} %param.21), kind=kOutput, calls=%fused_computation.4 | convolution fusion | flops 402751488 | bytes 12910592 | tf_op jit(solution)/shard_map/dot_general | solution.py:26
  14.3 0.3 reshape.125
  14.8 0.8 fusion.43
  16.0 2.5 %fusion.10 = bf16[32,16,512]{2,0,1:T(8,128)(2,1)S(1)} fusion(bf16[16,128,512]{2,1,0:T(8,128)(2,1)} %param.23, bf16[32,16,128]{2,1,0:T(8,128)(2,1)S(1)} %slice.37), kind=kOutput, calls=%fused_computation.19 | convolution fusion | flops 67371008 | bytes 2752512 | tf_op jit(solution)/shard_map/bhn,hnc->bhc/dot_general | solution.py:31
  18.5 0.1 subtract_convert_fusion
  18.7 0.4 fusion.16
  19.1 1.6 fusion.42
  20.7 0.3 fusion.22
  21.0 2.6 %fusion.28 = f32[32,16,576]{2,1,0:T(8,128)S(1)} fusion(bf16[32,256,576]{1,2,0:T(8,128)(2,1)S(1)} %copy-done.2, f32[32,16,256]{2,1,0:T(8,128)S(1)} %get-tuple-element.11, f32[32,16]{1,0:T(8,128)S(1)} %get-tuple-element.7, f32[32,16]{1,0:T(8,128)S(1)} %multiply_maximum_fusion), kind=kOutput, calls=%fused_computation.45 | convolution fusion | flops 151388160 | bytes 11145216 | tf_op jit(solution)/shard_map/bhl,blc->bhc/dot_general | solution.py:44
  23.6 0.2 fusion.15
  23.8 0.6 fusion.12
  24.4 0.7 slice-done.1
  25.1 2.2 %fusion.8 = bf16[32,2048]{1,0:T(8,128)(2,1)} fusion(bf16[2048,2048]{1,0:T(8,128)(2,1)S(1)} %bitcast.55, bf16[32,2048]{1,0:T(8,128)(2,1)S(1)} %copy-done.5, bf16[16,4,8,128]{3,2,1,0:T(8,128)(2,1)S(1)} %fusion.12), kind=kOutput, calls=%fused_computation.16 | convolution fusion | flops 268763136 | bytes 8781824 | tf_op jit(solution)/shard_map/dot_general | solution.py:47
  27.4 23.4 %all-gather.1 = f32[16,32,6]{1,2,0:T(8,128)S(1)} all-gather(f32[1,32,6]{1,2,0:T(8,128)S(1)} %bitcast.59), channel_id=1, replica_groups=mesh['dp'=2,'ep'=16] {'ep'}, dimensions={0}, use_global_device_ids=true | all-gather | bytes 13056 | tf_op jit(solution)/shard_map/all_gather | solution.py:84
  50.9 18.0 %all-gather = s32[16,32,6]{1,2,0:T(8,128)S(1)} all-gather(s32[1,32,6]{1,2,0:T(8,128)S(1)} %bitcast.60), channel_id=1, replica_groups=mesh['dp'=2,'ep'=16] {'ep'}, dimensions={0}, use_global_device_ids=true | all-gather | bytes 13056 | tf_op jit(solution)/shard_map/all_gather | solution.py:83
  69.5 2.6 %all-gather.4.cloned.1.call-done = bf16[512,2048]{1,0:T(8,128)(2,1)} async-done(((bf16[32,2048]{1,0:T(8,128)(2,1)}), bf16[512,2048]{1,0:T(8,128)(2,1)}) %all-gather.4.cloned.1.call-update) | async-done | bytes 2097168 | tf_op jit(solution)/shard_map/all_gather | solution.py:85
  72.1 3.3 %convolution_convert_fusion.2 = bf16[4,128,2048]{2,1,0:T(8,128)(2,1)S(1)} fusion(bf16[512,2048]{1,0:T(8,128)(2,1)} %all-gather.4.cloned.1.call-done, s32[4,512]{1,0:T(4,128)S(1)} %select_bitcast_fusion), kind=kOutput, calls=%fused_computation.6 | convolution fusion | flops 1075052544 | bytes 4202496 | tf_op jit(solution)/shard_map/est,th->esh/dot_general | solution.py:97
  75.4 9.4 %fusion.45 = f32[4,128,1408]{2,1,0:T(8,128)S(1)} fusion(bf16[4,128,2048]{2,1,0:T(8,128)(2,1)S(1)} %convolution_convert_fusion.2, bf16[4,2048,1408]{2,1,0:T(8,128)(2,1)} %param.29), kind=kOutput, calls=%fused_computation.81 | convolution fusion | flops 2952790016 | bytes 28049408 | tf_op jit(solution)/shard_map/gch,ghf->gcf/dot_general | solution.py:60
  84.9 12.6 %fusion.1 = bf16[4,128,1408]{2,1,0:T(8,128)(2,1)} fusion(bf16[4,128,2048]{2,1,0:T(8,128)(2,1)S(1)} %convolution_convert_fusion.2, bf16[4,2048,1408]{2,1,0:T(8,128)(2,1)} %param.30, f32[4,128,1408]{2,1,0:T(8,128)S(1)} %fusion.45), kind=kOutput, calls=%fused_computation.7 | convolution fusion | flops 2957115392 | bytes 29491200 | tf_op jit(solution)/shard_map/gch,ghf->gcf/dot_general | solution.py:61
  97.5 13.5 %multiply_reduce_fusion = f32[512,2048]{1,0:T(8,128)} fusion(f32[4,512]{1,0:T(4,128)S(1)} %bitcast.58, s32[4,512]{1,0:T(4,128)S(1)} %select_bitcast_fusion, bf16[4,128,1408]{2,1,0:T(8,128)(2,1)} %fusion.1, bf16[4,1408,2048]{2,1,0:T(8,128)(2,1)} %param.31), kind=kOutput, calls=%fused_computation | convolution fusion | flops 4035182592 | bytes 28721152 | tf_op jit(solution)/shard_map/est,esh->eth/dot_general | solution.py:99
  111.0 0.9 copy-done.3
  111.9 6.3 %fusion.44 = f32[32,2816]{1,0:T(8,128)S(1)} fusion(bf16[32,2048]{1,0:T(8,128)(2,1)S(1)} %copy-done.3, bf16[2048,2816]{1,0:T(8,128)(2,1)} %param.26), kind=kOutput, calls=%fused_computation.80 | convolution fusion | flops 369098752 | bytes 12025856 | tf_op jit(solution)/shard_map/dot_general | solution.py:53
  118.2 64.5 %reduce-scatter.2.cloned.1.call-done = f32[32,2048]{1,0:T(8,128)} async-done(((f32[512,2048]{1,0:T(8,128)}), f32[32,2048]{1,0:T(8,128)}) %reduce-scatter.2.cloned.1.call-update) | async-done | bytes 262160 | tf_op jit(solution)/shard_map/reduce_scatter | solution.py:101
  182.7 12.4 %fusion.5 = bf16[32,2048]{1,0:T(8,128)(2,1)} fusion(f32[32,2048]{1,0:T(8,128)} %reduce-scatter.2.cloned.1.call-done, bf16[2816,2048]{1,0:T(8,128)(2,1)} %param.28, bf16[32,2048]{1,0:T(8,128)(2,1)S(1)} %copy-done.3, bf16[2048,2816]{1,0:T(8,128)(2,1)} %param.27, f32[32,2816]{1,0:T(8,128)S(1)} %fusion.44), kind=kOutput, calls=%fused_computation.12 | convolution fusion | flops 739131392 | bytes 23953408 | tf_op jit(solution)/shard_map/dot_general | solution.py:56
  (53 shorter events, 1.6 us)
Async XLA Ops:
  7.2 7.6 %copy-start = (bf16[2048,576]{0,1:T(8,128)(2,1)S(1)}, bf16[2048,576]{0,1:T(8,128)(2,1)}, u32[]{:S(2)}) copy-start(bf16[2048,576]{0,1:T(8,128)(2,1)} %param.22) | copy-start | bytes 7077892
  7.2 65.0 %all-gather.4.cloned.1.call-start = ((), (), s32[]{:S(2)}) async-start(), calls=%async_computation.1 | async-start | bytes 2228224 | tf_op jit(solution)/shard_map/all_gather | solution.py:85
  7.2 7.5 %copy-start.9 = (s32[32]{0:T(128)S(1)}, s32[32]{0:T(128)}, u32[]{:S(2)}) copy-start(s32[32]{0:T(128)} %param.18) | copy-start | bytes 388
  7.3 7.6 %copy-start.5 = (bf16[32,2048]{1,0:T(8,128)(2,1)S(1)}, bf16[32,2048]{1,0:T(8,128)(2,1)}, u32[]{:S(2)}) copy-start(bf16[32,2048]{1,0:T(8,128)(2,1)} %param.16) | copy-start | bytes 393220
  14.8 4.3 %copy-start.2 = (bf16[32,256,576]{1,2,0:T(8,128)(2,1)S(1)}, bf16[32,256,576]{1,2,0:T(8,128)(2,1)}, u32[]{:S(2)}) copy-start(bf16[32,256,576]{1,2,0:T(8,128)(2,1)} %param.17) | copy-start | bytes 28311556
  15.9 7.7 %copy-start.6 = (bf16[32,576]{1,0:T(8,128)(2,1)}, bf16[32,576]{1,0:T(8,128)(2,1)S(1)}, u32[]{:S(2)}) copy-start(bf16[32,576]{1,0:T(8,128)(2,1)S(1)} %pad_maximum_fusion.1) | copy-start | bytes 110596
  21.0 3.4 %slice-start = ((s8[8388608]{0:T(1024)(128)(4,1)}), s8[4194304]{0:T(1024)(128)(4,1)S(1)}, s32[]{:S(2)}) async-start(s8[8388608]{0:T(1024)(128)(4,1)} %bitcast.54), calls=%async_computation.3 | async-start | bytes 8388608
  21.0 2.8 %copy-start.4 = (bf16[16,512,128]{2,1,0:T(8,128)(2,1)S(1)}, bf16[16,512,128]{2,1,0:T(8,128)(2,1)}, u32[]{:S(2)}) copy-start(bf16[16,512,128]{2,1,0:T(8,128)(2,1)} %param.24) | copy-start | bytes 6291460
  21.0 4.1 %slice-start.1 = ((s8[8388608]{0:T(1024)(128)(4,1)}), s8[4194304]{0:T(1024)(128)(4,1)S(1)}, s32[]{:S(2)}) async-start(s8[8388608]{0:T(1024)(128)(4,1)} %bitcast.54), calls=%async_computation.4 | async-start | bytes 8388608
  25.1 2.3 %copy-start.7 = (f32[32,6]{0,1:T(8,128)S(1)}, f32[32,6]{0,1:T(8,128)}, u32[]{:S(2)}) copy-start(f32[32,6]{0,1:T(8,128)} %param.20) | copy-start | bytes 2308
  25.1 25.8 %copy-start.8 = (s32[32,6]{0,1:T(8,128)S(1)}, s32[32,6]{0,1:T(8,128)}, u32[]{:S(2)}) copy-start(s32[32,6]{0,1:T(8,128)} %param.19) | copy-start | bytes 2308
  27.3 155.4 %reduce-scatter.2.cloned.1.call-start = ((), (), s32[]{:S(2)}) async-start(), calls=%async_computation.2 | async-start | bytes 4456448 | tf_op jit(solution)/shard_map/reduce_scatter | solution.py:101
  111.0 0.9 copy-start.3
  182.7 12.4 %copy-start.1 = (bf16[2048,576]{0,1:T(8,128)(2,1)S(1)}, bf16[2048,576]{0,1:T(8,128)(2,1)}, u32[]{:S(2)}) copy-start(bf16[2048,576]{0,1:T(8,128)(2,1)} %param.22) | copy-start | bytes 7077892
Sparse Core Ops, SparseCore 0:
  27.4 44.6 all-gather.3
  111.1 71.5 reduce-scatter.1

commit v2 on v0

--- a/solution.py
+++ b/solution.py
@@ -1,7 +1,15 @@
+import functools
+
 import jax
 import jax.numpy as jnp
 from jax import lax
+from jax.experimental import pallas as pl
+from jax.experimental.pallas import tpu as pltpu
 from jax.sharding import PartitionSpec as P
+
+MESH = pl.DeviceIdType.MESH
+BF = jnp.bfloat16
+F32 = jnp.float32
 
 
 def rotary(vec, cos_t, sin_t):
@@ -49,50 +57,305 @@
     return h_mid, kv_row
 
 
-def swiglu(rows_in, w_gate, w_up, w_down):
-    gate_val = jnp.dot(rows_in, w_gate, preferred_element_type=jnp.float32)
-    up_val = jnp.dot(rows_in, w_up, preferred_element_type=jnp.float32)
-    act_val = (jax.nn.silu(gate_val) * up_val).astype(jnp.bfloat16)
-    return jnp.dot(act_val, w_down, preferred_element_type=jnp.float32).astype(jnp.bfloat16)
-
-
-def expert_rows(row_buf, ex_gate, ex_up, ex_down):
-    gate_val = jnp.einsum("gch,ghf->gcf", row_buf, ex_gate, preferred_element_type=jnp.float32)
-    up_val = jnp.einsum("gch,ghf->gcf", row_buf, ex_up, preferred_element_type=jnp.float32)
-    act_val = (jax.nn.silu(gate_val) * up_val).astype(jnp.bfloat16)
-    return jnp.einsum("gcf,gfh->gch", act_val, ex_down, preferred_element_type=jnp.float32).astype(jnp.bfloat16)
-
-
-def expert_cap(seqs_dev, top_k, group_size, local_exp):
-    hot_devs = group_size // 4
-    pair_cap = (seqs_dev * ((3 * top_k) // 4) + hot_devs - 1) // hot_devs
-    return (pair_cap + local_exp - 1) // local_exp
+def route_meta(routes, route_gates, num_exp):
+    hit = routes[:, :, None] == jnp.arange(num_exp, dtype=jnp.int32)[None, None, :]
+    member = jnp.any(hit, axis=1)
+    gate_te = jnp.sum(jnp.where(hit, route_gates[:, :, None], 0.0), axis=1)
+    num_seq = routes.shape[0]
+    tri = (jnp.arange(num_seq)[:, None] > jnp.arange(num_seq)[None, :]).astype(BF)
+    rank = jnp.dot(tri, member.astype(BF), preferred_element_type=F32)
+    return jnp.concatenate([jnp.where(member, rank, -4096.0), gate_te], axis=1)
+
+
+NG = 5
+ND = 8
+NCH = 4
+
+
+def moe_kernel(h_ref, meta_ref, sg_ref, su_ref, sd_ref, eg_ref, eu_ref, ed_ref, out_ref,
+               gbuf, dbuf, h_all, meta_all, meta_t, sel, sel_t, gates, xe, act, act_sh, shared,
+               part, rc, ry, rz,
+               gsem, dsem, ag_send, ag_recv, am_send, am_recv,
+               s1_send, s1_recv, s2_send, s2_recv, s3_send, s3_recv):
+    me = lax.axis_index("ep")
+    c = lax.rem(me, 2)
+    y = lax.rem(lax.div(me, 2), 2)
+    z = lax.div(me, 4)
+    core_peer = me + 1 - 2 * c
+    y_peer = me + 2 - 4 * y
+    zs = [lax.rem(z + d, 4) for d in range(4)]
+    zback = [lax.rem(z + 4 - d, 4) for d in range(4)]
+    z_peers = [me + 4 * (zs[d] - z) for d in range(4)]
+    num_loc, hidden, ff = eg_ref.shape
+    num_seq = h_ref.shape[0]
+    cw = hidden // NCH
+
+    def g_copy(k):
+        slot = k % NG
+        if k < 4:
+            src = (sg_ref, su_ref)[k % 2].at[:, pl.ds((k // 2) * ff, ff)]
+        else:
+            src = (eg_ref, eu_ref)[k % 2].at[(k - 4) // 2]
+        return pltpu.make_async_copy(src, gbuf.at[slot], gsem.at[slot])
+
+    def d_copy(p):
+        slot = p % ND
+        if p < 8:
+            src = sd_ref.at[pl.ds((p % 2) * ff, ff), pl.ds((p // 2) * cw, cw)]
+        else:
+            q = p - 8
+            src = ed_ref.at[q % 4, :, pl.ds((q // 4) * cw, cw)]
+        return pltpu.make_async_copy(src, dbuf.at[slot], dsem.at[slot])
+
+    for k in range(4):
+        g_copy(k).start()
+    for p in range(ND):
+        d_copy(p).start()
+    g_copy(4).start()
+
+    barrier = pltpu.get_barrier_semaphore()
+    peers = [core_peer, y_peer, z_peers[1], z_peers[2], z_peers[3]]
+    for peer in peers:
+        pl.semaphore_signal(barrier, inc=1, device_id={"ep": peer}, device_id_type=MESH)
+    pl.semaphore_wait(barrier, len(peers))
+
+    def ag(src_pos, peer, n, own=False):
+        cc, yy, zz = src_pos
+        idx = (cc * 2 + yy) * 4 + zz
+        hb = h_ref if own else h_all.at[cc, yy, zz]
+        mb = meta_ref if own else meta_all.at[cc, yy, zz]
+        a = pltpu.make_async_remote_copy(src_ref=mb, dst_ref=meta_all.at[cc, yy, zz], send_sem=am_send.at[n], recv_sem=am_recv.at[idx], device_id={"ep": peer}, device_id_type=MESH)
+        b = pltpu.make_async_remote_copy(src_ref=hb, dst_ref=h_all.at[cc, yy, zz], send_sem=ag_send.at[n], recv_sem=ag_recv.at[idx], device_id={"ep": peer}, device_id_type=MESH)
+        return a, b
+
+    started = []
+
+    def send(src_pos, peer, n, own=False):
+        a, b = ag(src_pos, peer, n, own)
+        a.start()
+        b.start()
+        started.append((a, b))
+
+    def arrive(src_pos):
+        a, b = ag(src_pos, core_peer, 0)
+        a.wait_recv()
+        b.wait_recv()
+
+    mine = (c, y, z)
+    send(mine, y_peer, 0, True)
+    for d in (1, 2, 3):
+        send(mine, z_peers[d], d, True)
+    send(mine, core_peer, 4, True)
+    h_all[c, y, z] = h_ref[...]
+    meta_all[c, y, z] = meta_ref[...]
+
+    def fwd_z(d):
+        pos = (c, y, zback[d])
+        arrive(pos)
+        send(pos, y_peer, 4 + d)
+        send(pos, core_peer, 7 + d)
+
+    def fwd_y(d):
+        pos = (c, 1 - y, zback[d])
+        arrive(pos)
+        send(pos, core_peer, 11 + d)
+
+    def gate_up(x, gslot, uslot, store):
+        def block(start, size):
+            g = jnp.dot(x(), gbuf[gslot, :, pl.ds(start, size)], preferred_element_type=F32)
+            u = jnp.dot(x(), gbuf[uslot, :, pl.ds(start, size)], preferred_element_type=F32)
+            store(start, size, (g * jax.nn.sigmoid(g) * u).astype(BF))
+
+        @pl.loop(0, ff // 256)
+        def _(n):
+            block(pl.multiple_of(n * 256, 256), 256)
+
+        if ff % 256:
+            block(ff - ff % 256, ff % 256)
+
+    def g_wait(k):
+        g_copy(k).wait()
+
+    for s in range(2):
+        g_wait(2 * s)
+        g_wait(2 * s + 1)
+
+        def put(start, size, v, s=s):
+            act_sh[s, :, pl.ds(start, size)] = v
+        gate_up(lambda: h_ref[...], (2 * s) % NG, (2 * s + 1) % NG, put)
+        g_copy(2 * s + 5).start()
+        g_copy(2 * s + 6).start()
+        if s == 0:
+            fwd_z(1)
+            fwd_y(0)
+        else:
+            fwd_z(2)
+            fwd_z(3)
+    for j in range(NCH):
+        d_copy(2 * j).wait()
+        d_copy(2 * j + 1).wait()
+        o = jnp.dot(act_sh[0], dbuf[2 * j], preferred_element_type=F32) + jnp.dot(act_sh[1], dbuf[2 * j + 1], preferred_element_type=F32)
+        shared[:, j * cw:(j + 1) * cw] = o.astype(BF)
+        d_copy(2 * j + 8).start()
+        d_copy(2 * j + 9).start()
+        if j >= 1:
+            fwd_y(j)
+    for yy in range(2):
+        for zz in range(4):
+            arrive((1 - c, yy, zz))
+
+    ntok = 16 * num_seq
+    rows = 16 * 8
+    meta = meta_all[...].reshape(ntok, 128)
+    meta_t[...] = meta.T
+    lane = lax.broadcasted_iota(jnp.int32, (ntok, 128), 1)
+    base_col = lax.broadcasted_iota(jnp.int32, (ntok, 128), 0) // num_seq * 8
+    base_row = lax.broadcasted_iota(jnp.int32, (1, ntok), 1) // num_seq * 8
+    slot_row = lax.broadcasted_iota(jnp.int32, (rows, ntok), 0)
+    for e in range(num_loc):
+        ge = me * num_loc + e
+        code = jnp.sum(jnp.where(lane == ge, meta, 0.0), axis=1, keepdims=True)
+        gate = jnp.sum(jnp.where(lane == ge + 64, meta, 0.0), axis=1, keepdims=True)
+        sel[e] = jnp.where(lane == code.astype(jnp.int32) + base_col, 1.0, 0.0).astype(BF)
+        gates[e] = jnp.broadcast_to(gate, (ntok, 128))
+        code_t = meta_t[pl.ds(ge, 1), :].astype(jnp.int32) + base_row
+        sel_t[pl.ds(e * rows, rows), :] = jnp.where(slot_row == code_t, 1.0, 0.0).astype(BF)
+
+    @pl.loop(0, hidden // 512)
+    def _(n):
+        cols = pl.ds(pl.multiple_of(n * 512, 512), 512)
+        hh = h_all[:, :, :, :, cols].reshape(ntok, 512)
+        xe[:, cols] = jnp.dot(sel_t[...], hh, preferred_element_type=F32).astype(BF)
+
+    for e in range(num_loc):
+        g_wait(4 + 2 * e)
+        g_wait(5 + 2 * e)
+
+        def put(start, size, v, e=e):
+            act[e, :, pl.ds(start, size)] = v
+        gate_up(lambda e=e: xe[pl.ds(e * rows, rows), :], (4 + 2 * e) % NG, (5 + 2 * e) % NG, put)
+        for k in (9 + 2 * e, 10 + 2 * e):
+            if k < 4 + 2 * num_loc:
+                g_copy(k).start()
+
+    def s1(j):
+        cols = pl.ds(j * cw, cw)
+        return pltpu.make_async_remote_copy(src_ref=part.at[1 - c, :, :, :, cols], dst_ref=rc.at[:, :, :, cols], send_sem=s1_send.at[j], recv_sem=s1_recv.at[j], device_id={"ep": core_peer}, device_id_type=MESH)
+
+    def s2(j):
+        cols = pl.ds(j * cw, cw)
+        return pltpu.make_async_remote_copy(src_ref=part.at[c, 1 - y, :, :, cols], dst_ref=ry.at[:, :, cols], send_sem=s2_send.at[j], recv_sem=s2_recv.at[j], device_id={"ep": y_peer}, device_id_type=MESH)
+
+    def s3(j, d):
+        cols = pl.ds(j * cw, cw)
+        return pltpu.make_async_remote_copy(src_ref=part.at[c, y, zs[d], :, cols], dst_ref=rz.at[d - 1, :, cols], send_sem=s3_send.at[j * 3 + d - 1], recv_sem=s3_recv.at[j * 3 + d - 1], device_id={"ep": z_peers[d]}, device_id_type=MESH)
+
+    def after_s1(j):
+        cols = slice(j * cw, (j + 1) * cw)
+        s1(j).wait_recv()
+        part[c, 1 - y, :, :, cols] = part[c, 1 - y, :, :, cols] + rc[1 - y, :, :, cols]
+        s2(j).start()
+        part[c, y, :, :, cols] = part[c, y, :, :, cols] + rc[y, :, :, cols]
+
+    def after_s2(j):
+        cols = slice(j * cw, (j + 1) * cw)
+        s2(j).wait_recv()
+        part[c, y, :, :, cols] = part[c, y, :, :, cols] + ry[:, :, cols]
+        for d in (2, 1, 3):
+            s3(j, d).start()
+
+    def down(j):
+        cols = pl.ds(j * cw, cw)
+        for e in range(num_loc):
+            p = 8 + 4 * j + e
+            d_copy(p).wait()
+        for e in range(num_loc):
+            p = 8 + 4 * j + e
+            o = jnp.dot(act[e], dbuf[p % ND], preferred_element_type=F32).astype(BF)
+            if p + ND < 8 + 4 * NCH:
+                d_copy(p + ND).start()
+            for g in range(4):
+                tok = pl.ds(g * ntok // 4, ntok // 4)
+                b = jnp.dot(sel[e, tok, :], o, preferred_element_type=F32)
+                gt = gates[e, tok, :]
+                b = b * jnp.concatenate([gt] * (cw // 128), axis=1)
+                b = b.reshape(4, num_seq, cw)
+                if e == 0:
+                    part[g // 2, g % 2, :, :, cols] = b
+                else:
+                    part[g // 2, g % 2, :, :, cols] = part[g // 2, g % 2, :, :, cols] + b
+
+    for j in range(NCH):
+        down(j)
+        s1(j).start()
+        if j >= 1:
+            after_s1(j - 1)
+        if j >= 2:
+            after_s2(j - 2)
+    after_s1(NCH - 1)
+    after_s2(NCH - 2)
+    after_s2(NCH - 1)
+    for j in range(NCH):
+        cols = slice(j * cw, (j + 1) * cw)
+        for d in (1, 2, 3):
+            s3(j, d).wait_recv()
+        routed = part[c, y, z, :, cols] + rz[0, :, cols] + rz[1, :, cols] + rz[2, :, cols]
+        out_ref[:, cols] = (h_ref[:, cols].astype(F32) + shared[:, cols].astype(F32) + routed).astype(BF)
+    for a, b in started:
+        a.wait_send()
+        b.wait_send()
+    for j in range(NCH):
+        s1(j).wait_send()
+        s2(j).wait_send()
+        for d in (1, 2, 3):
+            s3(j, d).wait_send()
+
+
+def moe(h, meta, sh_gate, sh_up, sh_down, ex_gate, ex_up, ex_down):
+    num_seq, hidden = h.shape
+    num_loc, _, ff = ex_gate.shape
+    ntok = 16 * num_seq
+    dma = pltpu.SemaphoreType.DMA
+    vm = pl.BlockSpec(memory_space=pltpu.VMEM)
+    hbm = pl.BlockSpec(memory_space=pl.ANY)
+    return pl.pallas_call(
+        moe_kernel,
+        out_shape=jax.ShapeDtypeStruct((num_seq, hidden), BF),
+        in_specs=[vm, vm] + [hbm] * 6,
+        out_specs=vm,
+        scratch_shapes=[
+            pltpu.VMEM((NG, hidden, ff), BF),
+            pltpu.VMEM((ND, ff, hidden // NCH), BF),
+            pltpu.VMEM((2, 2, 4, num_seq, hidden), BF),
+            pltpu.VMEM((2, 2, 4, num_seq, 128), F32),
+            pltpu.VMEM((128, ntok), F32),
+            pltpu.VMEM((num_loc, ntok, 128), BF),
+            pltpu.VMEM((num_loc * 128, ntok), BF),
+            pltpu.VMEM((num_loc, ntok, 128), F32),
+            pltpu.VMEM((num_loc * 128, hidden), BF),
+            pltpu.VMEM((num_loc, 128, ff), BF),
+            pltpu.VMEM((2, num_seq, ff), BF),
+            pltpu.VMEM((num_seq, hidden), BF),
+            pltpu.VMEM((2, 2, 4, num_seq, hidden), F32),
+            pltpu.VMEM((2, 4, num_seq, hidden), F32),
+            pltpu.VMEM((4, num_seq, hidden), F32),
+            pltpu.VMEM((3, num_seq, hidden), F32),
+            dma((NG,)), dma((ND,)), dma((15,)), dma((16,)), dma((15,)), dma((16,)),
+            dma((NCH,)), dma((NCH,)), dma((NCH,)), dma((NCH,)), dma((3 * NCH,)), dma((3 * NCH,)),
+        ],
+        compiler_params=pltpu.CompilerParams(collective_id=0, has_side_effects=True, vmem_limit_bytes=67043328),
+        name="moe",
+    )(h, meta, sh_gate, sh_up, sh_down, ex_gate, ex_up, ex_down)
 
 
 def solution(mesh):
     group_size = mesh.shape["ep"]
 
     def device_step(x_blk, cache_blk, len_blk, routes, route_gates, w_q, w_dkv, w_uk, w_uv, w_o, sh_gate, sh_up, sh_down, ex_gate, ex_up, ex_down):
-        num_seq, hidden = x_blk.shape
-        top_k = routes.shape[1]
-        local_exp = ex_gate.shape[0]
-        num_exp = local_exp * group_size
-        exp_cap = expert_cap(num_seq, top_k, group_size, local_exp)
+        num_exp = ex_gate.shape[0] * group_size
+        meta = route_meta(routes, route_gates, num_exp)
         h_mid, kv_row = attend_local(x_blk, cache_blk, len_blk, w_q, w_dkv, w_uk, w_uv, w_o)
-        shared = swiglu(h_mid, sh_gate, sh_up, sh_down)
-        flat_ids = routes.reshape(-1)
-        onehot = (flat_ids[:, None] == jnp.arange(num_exp, dtype=jnp.int32)[None, :]).astype(jnp.int32)
-        rank_pos = jnp.sum((jnp.cumsum(onehot, axis=0) - onehot) * onehot, axis=1)
-        slot_idx = (flat_ids % local_exp) * (group_size * exp_cap) + (flat_ids // local_exp) * exp_cap + rank_pos
-        token_ids = jnp.arange(num_seq * top_k, dtype=jnp.int32) // top_k
-        slot_token = jnp.zeros((num_exp * exp_cap,), jnp.int32).at[slot_idx].set(token_ids)
-        send_buf = jnp.take(h_mid, slot_token, axis=0).reshape(local_exp, group_size, exp_cap, hidden)
-        recv_buf = lax.all_to_all(send_buf, "ep", 1, 1, tiled=True)
-        exp_out = expert_rows(recv_buf.reshape(local_exp, group_size * exp_cap, hidden), ex_gate, ex_up, ex_down)
-        back_buf = lax.all_to_all(exp_out.reshape(local_exp, group_size, exp_cap, hidden), "ep", 1, 1, tiled=True)
-        picked = jnp.take(back_buf.reshape(num_exp * exp_cap, hidden), slot_idx, axis=0).reshape(num_seq, top_k, hidden)
-        routed = jnp.sum(picked.astype(jnp.float32) * route_gates[:, :, None], axis=1)
-        layer_out = (h_mid.astype(jnp.float32) + shared.astype(jnp.float32) + routed).astype(jnp.bfloat16)
+        layer_out = moe(h_mid, meta, sh_gate, sh_up, sh_down, ex_gate, ex_up, ex_down)
         return layer_out, kv_row
 
     batch_spec = P(("dp", "ep"))

time: 191 us -> 108 us (0.57)
  the two profiles are of different devices: /device:TPU:15 before, /device:TPU:0 now
where the time goes in v2:
time: 108 us
  Pallas kernels  80.1 us (74%)
  matrix products  21.3 us (20%)
  local copies, waits for them, and re-layouts  2.84 us (3%)
  other arithmetic  2.69 us (2%)
    pallas_call x1, Pallas kernels, moe(): pl.pallas_call(moe_kernel, out_shape=jax.ShapeDtypeStruct((num_seq, hidde...  80.1 us
    dot_general x1, matrix products, attend_local(): jnp.dot(x_blk, w_q, preferred_element_type=jnp.float32).astype(jnp.bfloat16)  7.05 us
    dot_general x1, matrix products, attend_local(): jnp.einsum('bhc,blc->bhl', q_cat, cache_blk, preferred_element_type=jnp.f...  5.46 us
    dot_general x1, matrix products, attend_local(): jnp.einsum('bhl,blc->bhc', p_old, cache_blk, preferred_element_type=jnp.f...  2.56 us
    dot_general x1, matrix products, attend_local(): kv_raw = jnp.dot(x_blk, w_dkv, preferred_element_type=jnp.float32)  2.52 us
    unnamed x25, local copies, waits for them, and re-layouts  2.48 us
    dot_general x1, matrix products, attend_local(): jnp.dot(v_head.reshape(num_seq, num_heads * v_dim), w_o, preferred_elemen...  2.23 us

profile of v2, /device:TPU:0, one launch (start us, length us, event | category | flops | bytes accessed | tf_op | source)
XLA Modules:
  0.0 107.8 jit_solution(2124570335870985154)
XLA Ops:
  0.6 2.5 %fusion.23 = f32[32,576]{1,0:T(8,128)S(1)} fusion(bf16[32,2048]{1,0:T(8,128)(2,1)} %param.16, bf16[2048,576]{0,1:T(8,128)(2,1)} %param.22), kind=kOutput, calls=%fused_computation.51 | convolution fusion | flops 75497472 | bytes 2564096 | tf_op jit(solution)/shard_map/dot_general | solution.py:35
  3.2 0.7 convert_element_type.63
  3.8 0.1 subtract_convert_fusion.1
  4.0 7.0 %convolution_convert_fusion = bf16[32,3072]{1,0:T(8,128)(2,1)S(1)} fusion(bf16[32,2048]{1,0:T(8,128)(2,1)} %param.16, bf16[2048,3072]{1,0:T(8,128)(2,1)} %param.21), kind=kOutput, calls=%fused_computation | convolution fusion | flops 402751488 | bytes 12910592 | tf_op jit(solution)/shard_map/dot_general | solution.py:34
  11.1 0.3 reshape.109
  11.4 0.1 subtract_convert_fusion
  11.6 0.4 fusion.3
  12.0 0.1 pad_maximum_fusion
  12.3 0.4 fusion.7
  12.7 5.5 %fusion.22 = (f32[32,16]{1,0:T(8,128)S(1)}, f32[32,16,256]{2,1,0:T(8,128)S(1)}) fusion(bf16[32,256,576]{1,2,0:T(8,128)(2,1)} %param.17, bf16[32,16,576]{2,0,1:T(8,128)(2,1)S(1)} %pad_maximum_fusion, pred[32,256]{1,0:T(8,128)(4,1)S(1)} %iota_compare_fusion.1), kind=kOutput, calls=%fused_computation.50 | convolution fusion | flops 151387648 | bytes 10561536 | tf_op jit(solution)/shard_map/bhc,blc->bhl/dot_general | solution.py:42
  18.2 0.2 fusion.11
  18.5 0.2 slice-done.2
  18.7 2.6 %fusion.12 = f32[32,16,576]{2,1,0:T(8,128)S(1)} fusion(bf16[32,256,576]{1,2,0:T(8,128)(2,1)S(1)} %bitcast.23, f32[32,16,256]{2,1,0:T(8,128)S(1)} %get-tuple-element.11, f32[32,16]{1,0:T(8,128)S(1)} %get-tuple-element.7, f32[32,16]{1,0:T(8,128)S(1)} %multiply_maximum_fusion), kind=kOutput, calls=%fused_computation.22 | convolution fusion | flops 151388160 | bytes 11145216 | tf_op jit(solution)/shard_map/bhl,blc->bhc/dot_general | solution.py:52
  21.3 0.1 pad_maximum_fusion.1
  21.4 0.6 copy-done.3
  22.0 0.2 fusion.6
  22.2 0.6 fusion.5
  22.9 2.2 %fusion.2.h_ref = bf16[32,2048]{1,0:T(8,128)(2,1)} fusion(bf16[2048,2048]{1,0:T(8,128)(2,1)S(1)} %bitcast.25, bf16[32,2048]{1,0:T(8,128)(2,1)S(1)} %copy-done.2, bf16[16,4,8,128]{3,2,1,0:T(8,128)(2,1)S(1)} %fusion.5), kind=kOutput, calls=%fused_computation.4 | convolution fusion | flops 268763136 | bytes 8781824 | tf_op jit(solution)/shard_map/dot_general | solution.py:55
  25.1 0.1 fusion.18
  25.2 0.1 convolution_select_fusion
  25.3 0.1 select_reduce_fusion
  25.4 0.7 pad_maximum_fusion.2.meta_ref
  26.1 80.1 %moe.1 = bf16[32,2048]{1,0:T(8,128)(2,1)} custom-call(bf16[32,2048]{1,0:T(8,128)(2,1)} %fusion.2.h_ref, f32[32,128]{1,0:T(8,128)} %pad_maximum_fusion.2.meta_ref, bf16[2048,2816]{1,0:T(8,128)(2,1)} %sg_ref.1, bf16[2048,2816]{1,0:T(8,128)(2,1)} %su_ref.1, bf16[2816,2048]{1,0:T(8,128)(2,1)} %sd_ref.1, bf16[4,2048,1408]{2,1,0:T(8,128)(2,1)} %eg_ref.1, ...), custom_call_target="tpu_custom_call" | custom-call | tf_op jit(solution)/shard_map/moe/pallas_call | solution.py:321
  106.2 1.6 %copy.59 = bf16[32,2048]{1,0:T(8,128)(2,1)} copy(bf16[32,2048]{1,0:T(8,128)(2,1)} %moe.1) | data formatting | bytes 262144
  (34 shorter events, 0.4 us)
Async XLA Ops:
  4.0 7.6 %copy-start = (bf16[16,128,512]{2,1,0:T(8,128)(2,1)S(1)}, bf16[16,128,512]{2,1,0:T(8,128)(2,1)}, u32[]{:S(2)}) copy-start(bf16[16,128,512]{2,1,0:T(8,128)(2,1)} %param.23) | copy-start | bytes 6291460
  4.0 8.6 %copy-start.6 = (s32[32]{0:T(128)S(1)}, s32[32]{0:T(128)}, u32[]{:S(2)}) copy-start(s32[32]{0:T(128)} %param.18) | copy-start | bytes 388
  12.3 6.2 %slice-start = ((s8[9437184]{0:T(1024)(128)(4,1)}), s8[4194304]{0:T(1024)(128)(4,1)S(1)}, s32[]{:S(2)}) async-start(s8[9437184]{0:T(1024)(128)(4,1)} %bitcast.22), calls=%async_computation | async-start | bytes 8388608
  12.7 5.8 %slice-start.1 = ((s8[9437184]{0:T(1024)(128)(4,1)}), s8[4194304]{0:T(1024)(128)(4,1)S(1)}, s32[]{:S(2)}) async-start(s8[9437184]{0:T(1024)(128)(4,1)} %bitcast.22), calls=%async_computation.1 | async-start | bytes 8388608
  12.7 6.0 %slice-start.2 = ((s8[9437184]{0:T(1024)(128)(4,1)}), s8[1048576]{0:T(1024)(128)(4,1)S(1)}, s32[]{:S(2)}) async-start(s8[9437184]{0:T(1024)(128)(4,1)} %bitcast.22), calls=%async_computation.2 | async-start | bytes 2097152
  18.2 4.0 %copy-start.1 = (bf16[16,512,128]{2,1,0:T(8,128)(2,1)S(1)}, bf16[16,512,128]{2,1,0:T(8,128)(2,1)}, u32[]{:S(2)}) copy-start(bf16[16,512,128]{2,1,0:T(8,128)(2,1)} %param.24) | copy-start | bytes 6291460
  18.2 4.6 %slice-start.3 = ((s8[8388608]{0:T(1024)(128)(4,1)}), s8[4194304]{0:T(1024)(128)(4,1)S(1)}, s32[]{:S(2)}) async-start(s8[8388608]{0:T(1024)(128)(4,1)} %bitcast.24), calls=%async_computation.3 | async-start | bytes 8388608
  18.2 4.6 %copy-start.2 = (bf16[32,2048]{1,0:T(8,128)(2,1)S(1)}, bf16[32,2048]{1,0:T(8,128)(2,1)}, u32[]{:S(2)}) copy-start(bf16[32,2048]{1,0:T(8,128)(2,1)} %param.16) | copy-start | bytes 393220
  18.7 4.1 %slice-start.4 = ((s8[8388608]{0:T(1024)(128)(4,1)}), s8[4194304]{0:T(1024)(128)(4,1)S(1)}, s32[]{:S(2)}) async-start(s8[8388608]{0:T(1024)(128)(4,1)} %bitcast.24), calls=%async_computation.4 | async-start | bytes 8388608
  21.4 0.6 copy-start.3
  22.8 2.3 %copy-start.4 = (s32[32,6]{0,1:T(8,128)S(1)}, s32[32,6]{0,1:T(8,128)}, u32[]{:S(2)}) copy-start(s32[32,6]{0,1:T(8,128)} %param.19) | copy-start | bytes 2308
  22.9 2.5 %copy-start.5 = (f32[32,6]{0,1:T(8,128)S(1)}, f32[32,6]{0,1:T(8,128)}, u32[]{:S(2)}) copy-start(f32[32,6]{0,1:T(8,128)} %param.20) | copy-start | bytes 2308

commit v3 on v2

v3 whole, which is shorter than its diff:
```python
import functools

import jax
import jax.numpy as jnp
from jax import lax
from jax.experimental import pallas as pl
from jax.experimental.pallas import tpu as pltpu
from jax.sharding import PartitionSpec as P

MESH = pl.DeviceIdType.MESH
BF = jnp.bfloat16
F32 = jnp.float32


NG = 5
ND = 8
NCH = 4


def layer_kernel(x_ref, len_ref, routes_ref, rgate_ref, cache_ref, wq_ref, wdkv_ref, wuk_ref, wuv_ref, wo_ref,
                 sg_ref, su_ref, sd_ref, eg_ref, eu_ref, ed_ref, out_ref, kv_ref,
                 gbuf, dbuf, cbuf, dkv_buf, qn, kvf, vcat, h_own, meta_own,
                 h_all, meta_all, meta_t, sel, sel_t, gates, xe, act, act_sh, shared,
                 part, rc, ry, rz,
                 gsem, dsem, csem, xsem, ag_send, ag_recv, am_send, am_recv,
                 s1_send, s1_recv, s2_send, s2_recv, s3_send, s3_recv):
    me = lax.axis_index("ep")
    c = lax.rem(me, 2)
    y = lax.rem(lax.div(me, 2), 2)
    z = lax.div(me, 4)
    core_peer = me + 1 - 2 * c
    y_peer = me + 2 - 4 * y
    zs = [lax.rem(z + d, 4) for d in range(4)]
    zback = [lax.rem(z + 4 - d, 4) for d in range(4)]
    z_peers = [me + 4 * (zs[d] - z) for d in range(4)]
    num_loc, hidden, ff = eg_ref.shape
    num_seq = x_ref.shape[0]
    cw = hidden // NCH
    latent = wuk_ref.shape[1]
    num_heads = part.shape[0] * part.shape[1] * part.shape[2]
    nope = wuk_ref.shape[0] // num_heads
    rope = wdkv_ref.shape[1] - latent
    qw = nope + rope
    top_k = routes_ref.shape[1]

    W6 = 6 * qw
    W4 = 4 * qw
    OB = hidden - ff

    def g_copy(k):
        slot = k % NG
        dst = gbuf.at[slot]
        if k < 2:
            src, dst = wq_ref.at[:, pl.ds(k * W6, W6)], gbuf.at[slot, :, pl.ds(0, W6)]
        elif k == 2:
            src, dst = wq_ref.at[:, pl.ds(2 * W6, W4)], gbuf.at[slot, :, pl.ds(0, W4)]
        elif k == 3:
            src, dst = wo_ref.at[:, pl.ds(ff, OB)], gbuf.at[slot, :, pl.ds(0, OB)]
        elif k == 4:
            src = wo_ref.at[:, pl.ds(0, ff)]
        elif k < 9:
            src = (su_ref, sg_ref)[k % 2].at[:, pl.ds((k - 5) // 2 * ff, ff)]
        else:
            src = (eu_ref, eg_ref)[k % 2].at[(k - 9) // 2]
        return pltpu.make_async_copy(src, dst, gsem.at[slot])

    def uk_copy():
        return pltpu.make_async_copy(wuk_ref, gbuf.at[2, :, pl.ds(W4, latent)], xsem.at[0])

    def uv_copy(i):
        return pltpu.make_async_copy(wuv_ref.at[pl.ds(i * hidden, hidden)], gbuf.at[3, :, pl.ds(OB + 128 * i, 128)], xsem.at[1 + i])

    def dkv_copy():
        return pltpu.make_async_copy(wdkv_ref, dkv_buf, xsem.at[5])

    def c_copy(g, slot):
        return pltpu.make_async_copy(cache_ref.at[pl.ds(g * 8, 8)], cbuf.at[slot], csem.at[slot])

    def d_copy(p):
        slot = p % ND
        if p < 8:
            src = sd_ref.at[pl.ds((p % 2) * ff, ff), pl.ds((p // 2) * cw, cw)]
        else:
            q = p - 8
            src = ed_ref.at[q % 4, :, pl.ds((q // 4) * cw, cw)]
        return pltpu.make_async_copy(src, dbuf.at[slot], dsem.at[slot])

    g_copy(0).start()
    g_copy(1).start()
    g_copy(2).start()
    uk_copy().start()
    dkv_copy().start()
    c_copy(0, 0).start()
    c_copy(1, 1).start()
    g_copy(3).start()
    for i in range(4):
        uv_copy(i).start()
    g_copy(4).start()

    barrier = pltpu.get_barrier_semaphore()
    peers = [core_peer, y_peer, z_peers[1], z_peers[2], z_peers[3]]
    for peer in peers:
        pl.semaphore_signal(barrier, inc=1, device_id={"ep": peer}, device_id_type=MESH)

    lane = lax.broadcasted_iota(jnp.int32, (num_seq, 128), 1)
    member = jnp.zeros((num_seq, 128), F32)
    gate_te = jnp.zeros((num_seq, 128), F32)
    for k in range(top_k):
        hit = (lane % 64) == routes_ref[:, k:k + 1]
        member = jnp.where(hit, 1.0, member)
        gate_te = jnp.where(hit, rgate_ref[:, k:k + 1], gate_te)
    tri = jnp.where(lax.broadcasted_iota(jnp.int32, (num_seq, num_seq), 0) > lax.broadcasted_iota(jnp.int32, (num_seq, num_seq), 1), 1.0, 0.0)
    rank = jnp.dot(tri.astype(BF), member.astype(BF), preferred_element_type=F32)
    meta_own[...] = jnp.where(lane < 64, jnp.where(member > 0.5, rank, -4096.0), gate_te)

    freq = jnp.exp((lane % (rope // 2)).astype(F32) * (-2.0 * 9.210340371976184 / rope))
    angle = len_ref[...].astype(F32) * freq
    live = lane < rope
    cos_w = jnp.where(live, jnp.cos(angle), 0.0)
    sin_w = jnp.where(live, jnp.where(lane < rope // 2, -jnp.sin(angle), jnp.sin(angle)), 0.0)

    def rotate(v):
        turned = jnp.where(lane < rope // 2, pltpu.roll(v, 128 - rope // 2, 1), pltpu.roll(v, rope // 2, 1))
        return v * cos_w + turned * sin_w

    pl.semaphore_wait(barrier, len(peers))

    def ag(src_pos, peer, n, own, table):
        cc, yy, zz = src_pos
        idx = (cc * 2 + yy) * 4 + zz
        if table:
            mine_ref, all_ref, ss, rs = meta_own, meta_all, am_send, am_recv
        else:
            mine_ref, all_ref, ss, rs = h_own, h_all, ag_send, ag_recv
        return pltpu.make_async_remote_copy(src_ref=mine_ref if own else all_ref.at[cc, yy, zz], dst_ref=all_ref.at[cc, yy, zz], send_sem=ss.at[n], recv_sem=rs.at[idx], device_id={"ep": peer}, device_id_type=MESH)

    started = []

    def send(src_pos, peer, n, table, own=False):
        a = ag(src_pos, peer, n, own, table)
        a.start()
        started.append(a)

    def arrive(src_pos, table):
        ag(src_pos, core_peer, 0, False, table).wait_recv()

    mine = (c, y, z)

    def send_own(table):
        send(mine, y_peer, 0, table, True)
        for d in (1, 2, 3):
            send(mine, z_peers[d], d, table, True)
        send(mine, core_peer, 4, table, True)

    def fwd_z(d, table=False):
        pos = (c, y, zback[d])
        arrive(pos, table)
        send(pos, y_peer, 4 + d, table)
        send(pos, core_peer, 7 + d, table)

    def fwd_y(d, table=False):
        pos = (c, 1 - y, zback[d])
        arrive(pos, table)
        send(pos, core_peer, 11 + d, table)

    send_own(True)
    meta_all[c, y, z] = meta_own[...]

    def hidx(h):
        return h // 8, h // 4 % 2, h % 4

    def q_heads(k, first, count):
        g_copy(k).wait()
        qq = jnp.dot(x_ref[...], gbuf[k, :, pl.ds(0, count * qw)], preferred_element_type=F32).astype(BF).astype(F32)
        for i in range(count // 2):
            pair = qq[:, 2 * i * qw:2 * (i + 1) * qw]
            for h, v in ((first + 2 * i, pair), (first + 2 * i + 1, pltpu.roll(pair, qw, 1))):
                qn[h] = v[:, :nope].astype(BF)
                part[(*hidx(h), slice(None), pl.ds(latent, 128))] = rotate(v[:, nope:nope + 128])

    q_heads(0, 0, 6)
    g_copy(5).start()
    q_heads(1, 6, 6)
    g_copy(6).start()
    q_heads(2, 12, 4)
    uk_copy().wait()
    for h in range(num_heads):
        part[(*hidx(h), slice(None), pl.ds(0, latent))] = jnp.dot(qn[h], gbuf[2, pl.ds(h * nope, nope), pl.ds(W4, latent)], preferred_element_type=F32)
    g_copy(7).start()
    for d in (1, 2, 3):
        fwd_z(d, True)

    dkv_copy().wait()
    r = jnp.dot(x_ref[...], dkv_buf[...], preferred_element_type=F32)
    r_lat = r[:, :latent].astype(BF)
    r_rope = rotate(jnp.concatenate([r[:, latent:], jnp.zeros((num_seq, 128 - rope), F32)], axis=1)).astype(BF)
    kvf[:, :latent] = r_lat.astype(F32)
    kvf[:, latent:] = r_rope.astype(F32)
    kv_ref[:, :latent] = r_lat
    kv_ref[:, latent:] = r_rope[:, :rope]

    scale = qw ** -0.5
    nt = (((1,), (1,)), ((), ()))

    @pl.loop(0, num_seq // 8)
    def _(g):
        cs = lax.rem(g, 2)
        c_copy(g, cs).wait()
        rows8 = pl.ds(pl.multiple_of(g * 8, 8), 8)
        ql = part[:, :, :, rows8, pl.ds(0, latent)].reshape(128, latent).astype(BF)
        qr = part[:, :, :, rows8, pl.ds(latent, 128)].reshape(128, 128)[:, :rope].astype(BF)
        kv8 = kvf[rows8, :]
        lane8 = lax.broadcasted_iota(jnp.int32, (8, 128), 1)
        diag = lane8 % 8 == lax.broadcasted_iota(jnp.int32, (8, 128), 0)
        nrow = jnp.sum(jnp.where(diag, len_ref[rows8, :].astype(F32), 0.0), axis=0, keepdims=True)
        sn = lax.dot_general(kv8[:, :latent].astype(BF), ql, nt, preferred_element_type=F32) + lax.dot_general(kv8[:, latent:latent + rope].astype(BF), qr, nt, preferred_element_type=F32)
        s_new = jnp.sum(jnp.where(diag, sn, 0.0), axis=0, keepdims=True) * scale
        lane_l = lax.broadcasted_iota(jnp.int32, (256, 128), 1) % 8
        s = jnp.zeros((256, 128), F32)
        for half in range(2):
            kl = cbuf[cs, pl.ds(4 * half, 4), :, pl.ds(0, latent)].reshape(1024, latent)
            kr = cbuf[cs, pl.ds(4 * half, 4), :, pl.ds(latent, rope)].reshape(1024, rope)
            big = lax.dot_general(kl, ql, nt, preferred_element_type=F32) + lax.dot_general(kr, qr, nt, preferred_element_type=F32)
            for b in range(4):
                s = jnp.where(lane_l == 4 * half + b, big[b * 256:(b + 1) * 256], s)
        row_l = lax.broadcasted_iota(jnp.int32, (256, 128), 0).astype(F32)
        s = jnp.where(row_l < nrow, s * scale, -jnp.inf)
        top = jnp.maximum(jnp.max(s, axis=0, keepdims=True), s_new)
        e = jnp.exp(s - top)
        e_new = jnp.exp(s_new - top)
        den = jnp.sum(e, axis=0, keepdims=True) + e_new
        p = (e / den).T
        p_new = jnp.broadcast_to((e_new / den).astype(BF).astype(F32), (128, 128)).T
        row_p = lax.broadcasted_iota(jnp.int32, (128, 256), 0) % 8
        p_big = jnp.concatenate([jnp.where(row_p == b, p, 0.0).astype(BF) for b in range(8)], axis=1)
        o = jnp.dot(p_big, cbuf[cs, :, :, pl.ds(0, latent)].reshape(2048, latent), preferred_element_type=F32)
        kv_rep = jnp.broadcast_to(kv8[None, :, :latent], (16, 8, latent)).reshape(128, latent)
        o = o + jnp.concatenate([p_new] * (latent // 128), axis=1) * kv_rep
        part[:, :, :, rows8, pl.ds(1024, latent)] = o.reshape(2, 2, 4, 8, latent)

        @pl.when(g + 2 < num_seq // 8)
        def _():
            c_copy(g + 2, cs).start()

    for p in range(ND):
        d_copy(p).start()
    for d in range(4):
        fwd_y(d, True)
    for i in range(4):
        uv_copy(i).wait()
    g_copy(3).wait()
    for h in range(num_heads):
        ob = part[(*hidx(h), slice(None), pl.ds(1024, latent))].astype(BF)
        vcat[:, h * 128:(h + 1) * 128] = jnp.dot(ob, gbuf[3, pl.ds(h % 4 * latent, latent), pl.ds(OB + 128 * (h // 4), 128)], preferred_element_type=F32).astype(BF)
    g_copy(4).wait()
    for lo, hi, slot in ((0, ff, 4), (ff, hidden, 3)):
        a = jnp.dot(vcat[...], gbuf[slot, :, pl.ds(0, hi - lo)], preferred_element_type=F32).astype(BF)
        h_own[:, lo:hi] = (x_ref[:, lo:hi].astype(F32) + a.astype(F32)).astype(BF)
    g_copy(8).start()
    g_copy(9).start()
    send_own(False)
    h_all[c, y, z] = h_own[...]

    def gate_up(x, gslot, uslot, store):
        def block(start, size):
            g = jnp.dot(x(), gbuf[gslot, :, pl.ds(start, size)], preferred_element_type=F32)
            u = jnp.dot(x(), gbuf[uslot, :, pl.ds(start, size)], preferred_element_type=F32)
            store(start, size, (g * jax.nn.sigmoid(g) * u).astype(BF))

        @pl.loop(0, ff // 256)
        def _(n):
            block(pl.multiple_of(n * 256, 256), 256)

        if ff % 256:
            block(ff - ff % 256, ff % 256)

    def g_wait(k):
        g_copy(k).wait()

    for s in range(2):
        g_wait(2 * s + 5)
        g_wait(2 * s + 6)

        def put(start, size, v, s=s):
            act_sh[s, :, pl.ds(start, size)] = v
        gate_up(lambda: h_own[...], (2 * s + 5) % NG, (2 * s + 6) % NG, put)
        g_copy(2 * s + 10).start()
        g_copy(2 * s + 11).start()
        if s == 0:
            fwd_z(1)
            fwd_y(0)
        else:
            fwd_z(2)
            fwd_z(3)
    for j in range(NCH):
        d_copy(2 * j).wait()
        d_copy(2 * j + 1).wait()
        o = jnp.dot(act_sh[0], dbuf[2 * j], preferred_element_type=F32) + jnp.dot(act_sh[1], dbuf[2 * j + 1], preferred_element_type=F32)
        shared[:, j * cw:(j + 1) * cw] = o.astype(BF)
        d_copy(2 * j + 8).start()
        d_copy(2 * j + 9).start()
        if j >= 1:
            fwd_y(j)
    for yy in range(2):
        for zz in range(4):
            arrive((1 - c, yy, zz), True)
            arrive((1 - c, yy, zz), False)

    ntok = 16 * num_seq
    rows = 16 * 8
    meta = meta_all[...].reshape(ntok, 128)
    meta_t[...] = meta.T
    lane = lax.broadcasted_iota(jnp.int32, (ntok, 128), 1)
    base_col = lax.broadcasted_iota(jnp.int32, (ntok, 128), 0) // num_seq * 8
    base_row = lax.broadcasted_iota(jnp.int32, (1, ntok), 1) // num_seq * 8
    slot_row = lax.broadcasted_iota(jnp.int32, (rows, ntok), 0)
    for e in range(num_loc):
        ge = me * num_loc + e
        code = jnp.sum(jnp.where(lane == ge, meta, 0.0), axis=1, keepdims=True)
        gate = jnp.sum(jnp.where(lane == ge + 64, meta, 0.0), axis=1, keepdims=True)
        sel[e] = jnp.where(lane == code.astype(jnp.int32) + base_col, 1.0, 0.0).astype(BF)
        gates[e] = jnp.broadcast_to(gate, (ntok, 128))
        code_t = meta_t[pl.ds(ge, 1), :].astype(jnp.int32) + base_row
        sel_t[pl.ds(e * rows, rows), :] = jnp.where(slot_row == code_t, 1.0, 0.0).astype(BF)

    @pl.loop(0, hidden // 512)
    def _(n):
        cols = pl.ds(pl.multiple_of(n * 512, 512), 512)
        hh = h_all[:, :, :, :, cols].reshape(ntok, 512)
        xe[:, cols] = jnp.dot(sel_t[...], hh, preferred_element_type=F32).astype(BF)

    for e in range(num_loc):
        g_wait(9 + 2 * e)
        g_wait(10 + 2 * e)

        def put(start, size, v, e=e):
            act[e, :, pl.ds(start, size)] = v
        gate_up(lambda e=e: xe[pl.ds(e * rows, rows), :], (9 + 2 * e) % NG, (10 + 2 * e) % NG, put)
        for k in (14 + 2 * e, 15 + 2 * e):
            if k < 9 + 2 * num_loc:
                g_copy(k).start()

    def s1(j):
        cols = pl.ds(j * cw, cw)
        return pltpu.make_async_remote_copy(src_ref=part.at[1 - c, :, :, :, cols], dst_ref=rc.at[:, :, :, cols], send_sem=s1_send.at[j], recv_sem=s1_recv.at[j], device_id={"ep": core_peer}, device_id_type=MESH)

    def s2(j):
        cols = pl.ds(j * cw, cw)
        return pltpu.make_async_remote_copy(src_ref=part.at[c, 1 - y, :, :, cols], dst_ref=ry.at[:, :, cols], send_sem=s2_send.at[j], recv_sem=s2_recv.at[j], device_id={"ep": y_peer}, device_id_type=MESH)

    def s3(j, d):
        cols = pl.ds(j * cw, cw)
        return pltpu.make_async_remote_copy(src_ref=part.at[c, y, zs[d], :, cols], dst_ref=rz.at[d - 1, :, cols], send_sem=s3_send.at[j * 3 + d - 1], recv_sem=s3_recv.at[j * 3 + d - 1], device_id={"ep": z_peers[d]}, device_id_type=MESH)

    def after_s1(j):
        cols = slice(j * cw, (j + 1) * cw)
        s1(j).wait_recv()
        part[c, 1 - y, :, :, cols] = part[c, 1 - y, :, :, cols] + rc[1 - y, :, :, cols]
        s2(j).start()
        part[c, y, :, :, cols] = part[c, y, :, :, cols] + rc[y, :, :, cols]

    def after_s2(j):
        cols = slice(j * cw, (j + 1) * cw)
        s2(j).wait_recv()
        part[c, y, :, :, cols] = part[c, y, :, :, cols] + ry[:, :, cols]
        for d in (2, 1, 3):
            s3(j, d).start()

    def down(j):
        cols = pl.ds(j * cw, cw)
        for e in range(num_loc):
            p = 8 + 4 * j + e
            d_copy(p).wait()
        for e in range(num_loc):
            p = 8 + 4 * j + e
            o = jnp.dot(act[e], dbuf[p % ND], preferred_element_type=F32).astype(BF)
            if p + ND < 8 + 4 * NCH:
                d_copy(p + ND).start()
            for g in range(4):
                tok = pl.ds(g * ntok // 4, ntok // 4)
                b = jnp.dot(sel[e, tok, :], o, preferred_element_type=F32)
                gt = gates[e, tok, :]
                b = b * jnp.concatenate([gt] * (cw // 128), axis=1)
                b = b.reshape(4, num_seq, cw)
                if e == 0:
                    part[g // 2, g % 2, :, :, cols] = b
                else:
                    part[g // 2, g % 2, :, :, cols] = part[g // 2, g % 2, :, :, cols] + b

    for j in range(NCH):
        down(j)
        s1(j).start()
        if j >= 1:
            after_s1(j - 1)
        if j >= 2:
            after_s2(j - 2)
    after_s1(NCH - 1)
    after_s2(NCH - 2)
    after_s2(NCH - 1)
    for j in range(NCH):
        cols = slice(j * cw, (j + 1) * cw)
        for d in (1, 2, 3):
            s3(j, d).wait_recv()
        routed = part[c, y, z, :, cols] + rz[0, :, cols] + rz[1, :, cols] + rz[2, :, cols]
        out_ref[:, cols] = (h_own[:, cols].astype(F32) + shared[:, cols].astype(F32) + routed).astype(BF)
    for a in started:
        a.wait_send()
    for j in range(NCH):
        s1(j).wait_send()
        s2(j).wait_send()
        for d in (1, 2, 3):
            s3(j, d).wait_send()


def layer(x, lens, routes, route_gates, cache, w_q, w_dkv, w_uk, w_uv, w_o, sh_gate, sh_up, sh_down, ex_gate, ex_up, ex_down):
    num_seq, hidden = x.shape
    num_loc, _, ff = ex_gate.shape
    lat_row = cache.shape[2]
    ntok = 16 * num_seq
    dma = pltpu.SemaphoreType.DMA
    vm = pl.BlockSpec(memory_space=pltpu.VMEM)
    hbm = pl.BlockSpec(memory_space=pl.ANY)
    return pl.pallas_call(
        layer_kernel,
        out_shape=(jax.ShapeDtypeStruct((num_seq, hidden), BF), jax.ShapeDtypeStruct((num_seq, lat_row), BF)),
        in_specs=[vm] * 4 + [hbm] * 12,
        out_specs=(vm, vm),
        scratch_shapes=[
            pltpu.VMEM((NG, hidden, ff), BF),
            pltpu.VMEM((ND, ff, hidden // NCH), BF),
            pltpu.VMEM((2, 8, cache.shape[1], lat_row), BF),
            pltpu.VMEM((hidden, lat_row), BF),
            pltpu.VMEM((16, num_seq, 128), BF),
            pltpu.VMEM((num_seq, 640), F32),
            pltpu.VMEM((num_seq, hidden), BF),
            pltpu.VMEM((num_seq, hidden), BF),
            pltpu.VMEM((num_seq, 128), F32),
            pltpu.VMEM((2, 2, 4, num_seq, hidden), BF),
            pltpu.VMEM((2, 2, 4, num_seq, 128), F32),
            pltpu.VMEM((128, ntok), F32),
            pltpu.VMEM((num_loc, ntok, 128), BF),
            pltpu.VMEM((num_loc * 128, ntok), BF),
            pltpu.VMEM((num_loc, ntok, 128), F32),
            pltpu.VMEM((num_loc * 128, hidden), BF),
            pltpu.VMEM((num_loc, 128, ff), BF),
            pltpu.VMEM((2, num_seq, ff), BF),
            pltpu.VMEM((num_seq, hidden), BF),
            pltpu.VMEM((2, 2, 4, num_seq, hidden), F32),
            pltpu.VMEM((2, 4, num_seq, hidden), F32),
            pltpu.VMEM((4, num_seq, hidden), F32),
            pltpu.VMEM((3, num_seq, hidden), F32),
            dma((NG,)), dma((ND,)), dma((2,)), dma((6,)), dma((15,)), dma((16,)), dma((15,)), dma((16,)),
            dma((NCH,)), dma((NCH,)), dma((NCH,)), dma((NCH,)), dma((3 * NCH,)), dma((3 * NCH,)),
        ],
        compiler_params=pltpu.CompilerParams(collective_id=0, has_side_effects=True, vmem_limit_bytes=67043328),
        name="layer",
    )(x, lens, routes, route_gates, cache, w_q, w_dkv, w_uk, w_uv, w_o, sh_gate, sh_up, sh_down, ex_gate, ex_up, ex_down)


def solution(mesh):
    def device_step(x_blk, cache_blk, len_blk, routes, route_gates, w_q, w_dkv, w_uk, w_uv, w_o, sh_gate, sh_up, sh_down, ex_gate, ex_up, ex_down):
        lens = jnp.broadcast_to(len_blk[:, None], (len_blk.shape[0], 128))
        uk = w_uk.reshape(-1, w_uk.shape[2])
        uv = w_uv.reshape(-1, w_uv.shape[2])
        return layer(x_blk, lens, routes, route_gates, cache_blk, w_q, w_dkv, uk, uv, w_o, sh_gate, sh_up, sh_down, ex_gate, ex_up, ex_down)

    batch_spec = P(("dp", "ep"))
    weight_spec = P()
    expert_spec = P("ep")
    in_specs = (batch_spec,) * 5 + (weight_spec,) * 8 + (expert_spec,) * 3
    return jax.shard_map(device_step, mesh=mesh, in_specs=in_specs, out_specs=(batch_spec, batch_spec), check_vma=False)
```

time: 108 us -> 125 us (1.16)
  local copies, waits for them, and re-layouts: 2.84 us -> 25.8 us
  matrix products: 21.3 us -> 0 us
  Pallas kernels: 80.1 us -> 98.2 us
  other arithmetic: 2.69 us -> 0 us
    unnamed x25 -> x6, local copies, waits for them, and re-layouts: 2.48 us -> 24.5 us
    dot_general x9 -> x0, matrix products: 21.3 us -> none  [the longest x1 7.05 us: attend_local(): jnp.dot(x_blk, w_q, preferred_element_type=jnp.float32).astype(jnp.bfloat16)]
    pallas_call x1, Pallas kernels: 80.1 us -> 98.2 us  [layer(): pl.pallas_call(layer_kernel, out_shape=(jax.ShapeDtypeStruct((num_seq, hi...]
    broadcast_in_dim x0 -> x1, local copies, waits for them, and re-layouts: none -> 1.33 us  [device_step(): lens = jnp.broadcast_to(len_blk[:, None], (len_blk.shape[0], 128))]
where the time goes in v3:
time: 125 us
  Pallas kernels  98.2 us (79%)
  local copies, waits for them, and re-layouts  25.8 us (21%)
    pallas_call x1, Pallas kernels, layer(): pl.pallas_call(layer_kernel, out_shape=(jax.ShapeDtypeStruct((num_seq, hi...  98.2 us
    unnamed x6, local copies, waits for them, and re-layouts  24.5 us

profile of v3, /device:TPU:0, one launch (start us, length us, event | category | flops | bytes accessed | tf_op | source)
XLA Modules:
  0.0 124.7 jit_solution(10262701608753489512)
XLA Ops:
  0.6 1.3 %broadcast_in_dim.2.len_ref = s32[32,128]{1,0:T(8,128)} broadcast(s32[32]{0:T(128)} %param.18), dimensions={0} | broadcast | bytes 16512 | tf_op jit(solution)/shard_map/broadcast_in_dim | solution.py:462
  2.0 1.4 %copy.18.routes_ref = s32[32,6]{1,0:T(8,128)} copy(s32[32,6]{0,1:T(8,128)} %param.19) | data formatting | bytes 1536 | tf_op args[3]
  3.3 1.4 %copy.19.rgate_ref = f32[32,6]{1,0:T(8,128)} copy(f32[32,6]{0,1:T(8,128)} %param.20) | data formatting | bytes 1536 | tf_op args[4]
  4.7 4.4 %copy.21.wdkv_ref = bf16[2048,576]{1,0:T(8,128)(2,1)} copy(bf16[2048,576]{0,1:T(8,128)(2,1)} %param.22) | data formatting | bytes 4718592 | tf_op args[6]
  9.1 14.4 %copy.20.cache_ref = bf16[32,256,576]{2,1,0:T(8,128)(2,1)} copy(bf16[32,256,576]{1,2,0:T(8,128)(2,1)} %param.17) | data formatting | bytes 18874368 | tf_op args[1]
  23.5 98.2 %layer.1 = (bf16[32,2048]{1,0:T(8,128)(2,1)}, bf16[32,576]{1,0:T(8,128)(2,1)}) custom-call(bf16[32,2048]{1,0:T(8,128)(2,1)} %x_ref.1, s32[32,128]{1,0:T(8,128)} %broadcast_in_dim.2.len_ref, s32[32,6]{1,0:T(8,128)} %copy.18.routes_ref, f32[32,6]{1,0:T(8,128)} %copy.19.rgate_ref, bf16[32,256,576]{2,1,0:T(8,128)(2,1)} %copy.20.cache_ref, ...), custom_call_target="tpu_custom_call" | custom-call | tf_op jit(solution)/shard_map/layer/pallas_call | solution.py:423
  121.7 1.6 %copy.24 = bf16[32,2048]{1,0:T(8,128)(2,1)} copy(bf16[32,2048]{1,0:T(8,128)(2,1)} %get-tuple-element.4) | data formatting | bytes 262144
  123.3 1.4 %copy.25 = bf16[32,576]{1,0:T(8,128)(2,1)} copy(bf16[32,576]{1,0:T(8,128)(2,1)} %get-tuple-element.5) | data formatting | bytes 73728

commit v4 on v3

--- a/solution.py
+++ b/solution.py
@@ -19,7 +19,7 @@
 
 def layer_kernel(x_ref, len_ref, routes_ref, rgate_ref, cache_ref, wq_ref, wdkv_ref, wuk_ref, wuv_ref, wo_ref,
                  sg_ref, su_ref, sd_ref, eg_ref, eu_ref, ed_ref, out_ref, kv_ref,
-                 gbuf, dbuf, cbuf, dkv_buf, qn, kvf, vcat, h_own, meta_own,
+                 gbuf, dbuf, cbuf, dkv_buf, qn, kvf, lenb, vcat, h_own, meta_own,
                  h_all, meta_all, meta_t, sel, sel_t, gates, xe, act, act_sh, shared,
                  part, rc, ry, rz,
                  gsem, dsem, csem, xsem, ag_send, ag_recv, am_send, am_recv,
@@ -39,9 +39,9 @@
     latent = wuk_ref.shape[1]
     num_heads = part.shape[0] * part.shape[1] * part.shape[2]
     nope = wuk_ref.shape[0] // num_heads
-    rope = wdkv_ref.shape[1] - latent
+    rope = wdkv_ref.shape[0] - latent
     qw = nope + rope
-    top_k = routes_ref.shape[1]
+    top_k = routes_ref.shape[0]
 
     W6 = 6 * qw
     W4 = 4 * qw
@@ -103,18 +103,23 @@
         pl.semaphore_signal(barrier, inc=1, device_id={"ep": peer}, device_id_type=MESH)
 
     lane = lax.broadcasted_iota(jnp.int32, (num_seq, 128), 1)
+    pad_k = jnp.zeros((8 - top_k, num_seq), F32)
+    small = jnp.concatenate([routes_ref[...].astype(F32), pad_k, rgate_ref[...], pad_k, len_ref[...].astype(F32), jnp.zeros((15, num_seq), F32)], axis=0)
+    small = jnp.concatenate([small, jnp.zeros((32, 128 - num_seq), F32)], axis=1)
+    cols = jnp.concatenate([small, jnp.zeros((96, 128), F32)], axis=0).T[:num_seq]
+    lenb[...] = jnp.broadcast_to(cols[:, 16:17], (num_seq, 128))
     member = jnp.zeros((num_seq, 128), F32)
     gate_te = jnp.zeros((num_seq, 128), F32)
     for k in range(top_k):
-        hit = (lane % 64) == routes_ref[:, k:k + 1]
+        hit = (lane % 64).astype(F32) == cols[:, k:k + 1]
         member = jnp.where(hit, 1.0, member)
-        gate_te = jnp.where(hit, rgate_ref[:, k:k + 1], gate_te)
+        gate_te = jnp.where(hit, cols[:, 8 + k:9 + k], gate_te)
     tri = jnp.where(lax.broadcasted_iota(jnp.int32, (num_seq, num_seq), 0) > lax.broadcasted_iota(jnp.int32, (num_seq, num_seq), 1), 1.0, 0.0)
     rank = jnp.dot(tri.astype(BF), member.astype(BF), preferred_element_type=F32)
     meta_own[...] = jnp.where(lane < 64, jnp.where(member > 0.5, rank, -4096.0), gate_te)
 
     freq = jnp.exp((lane % (rope // 2)).astype(F32) * (-2.0 * 9.210340371976184 / rope))
-    angle = len_ref[...].astype(F32) * freq
+    angle = lenb[...] * freq
     live = lane < rope
     cos_w = jnp.where(live, jnp.cos(angle), 0.0)
     sin_w = jnp.where(live, jnp.where(lane < rope // 2, -jnp.sin(angle), jnp.sin(angle)), 0.0)
@@ -190,8 +195,9 @@
     for d in (1, 2, 3):
         fwd_z(d, True)
 
+    nt = (((1,), (1,)), ((), ()))
     dkv_copy().wait()
-    r = jnp.dot(x_ref[...], dkv_buf[...], preferred_element_type=F32)
+    r = lax.dot_general(x_ref[...], dkv_buf[...], nt, preferred_element_type=F32)
     r_lat = r[:, :latent].astype(BF)
     r_rope = rotate(jnp.concatenate([r[:, latent:], jnp.zeros((num_seq, 128 - rope), F32)], axis=1)).astype(BF)
     kvf[:, :latent] = r_lat.astype(F32)
@@ -200,42 +206,32 @@
     kv_ref[:, latent:] = r_rope[:, :rope]
 
     scale = qw ** -0.5
-    nt = (((1,), (1,)), ((), ()))
 
     @pl.loop(0, num_seq // 8)
     def _(g):
         cs = lax.rem(g, 2)
         c_copy(g, cs).wait()
         rows8 = pl.ds(pl.multiple_of(g * 8, 8), 8)
-        ql = part[:, :, :, rows8, pl.ds(0, latent)].reshape(128, latent).astype(BF)
-        qr = part[:, :, :, rows8, pl.ds(latent, 128)].reshape(128, 128)[:, :rope].astype(BF)
-        kv8 = kvf[rows8, :]
-        lane8 = lax.broadcasted_iota(jnp.int32, (8, 128), 1)
-        diag = lane8 % 8 == lax.broadcasted_iota(jnp.int32, (8, 128), 0)
-        nrow = jnp.sum(jnp.where(diag, len_ref[rows8, :].astype(F32), 0.0), axis=0, keepdims=True)
-        sn = lax.dot_general(kv8[:, :latent].astype(BF), ql, nt, preferred_element_type=F32) + lax.dot_general(kv8[:, latent:latent + rope].astype(BF), qr, nt, preferred_element_type=F32)
-        s_new = jnp.sum(jnp.where(diag, sn, 0.0), axis=0, keepdims=True) * scale
-        lane_l = lax.broadcasted_iota(jnp.int32, (256, 128), 1) % 8
-        s = jnp.zeros((256, 128), F32)
-        for half in range(2):
-            kl = cbuf[cs, pl.ds(4 * half, 4), :, pl.ds(0, latent)].reshape(1024, latent)
-            kr = cbuf[cs, pl.ds(4 * half, 4), :, pl.ds(latent, rope)].reshape(1024, rope)
-            big = lax.dot_general(kl, ql, nt, preferred_element_type=F32) + lax.dot_general(kr, qr, nt, preferred_element_type=F32)
-            for b in range(4):
-                s = jnp.where(lane_l == 4 * half + b, big[b * 256:(b + 1) * 256], s)
-        row_l = lax.broadcasted_iota(jnp.int32, (256, 128), 0).astype(F32)
-        s = jnp.where(row_l < nrow, s * scale, -jnp.inf)
-        top = jnp.maximum(jnp.max(s, axis=0, keepdims=True), s_new)
+        q = part[:, :, :, rows8, pl.ds(0, latent + 128)].reshape(128, latent + 128).astype(BF)
+        kv_rep = jnp.broadcast_to(kvf[rows8, :][None], (16, 8, latent + 128)).reshape(128, latent + 128)
+        n_rep = jnp.broadcast_to(lenb[rows8, :][None], (16, 8, 128)).reshape(128, 128)
+        n_rep = jnp.concatenate([n_rep, n_rep], axis=1)
+        row = lax.broadcasted_iota(jnp.int32, (128, 256), 0) % 8
+        pos = lax.broadcasted_iota(jnp.int32, (128, 256), 1).astype(F32)
+        s_new = jnp.sum(q.astype(F32) * kv_rep, axis=1, keepdims=True) * scale
+        q = q[:, :latent + rope]
+        s = jnp.zeros((128, 256), F32)
+        for b in range(8):
+            s = jnp.where(row == b, jnp.dot(q, cbuf[cs, b], preferred_element_type=F32), s)
+        s = jnp.where(pos < n_rep, s * scale, -jnp.inf)
+        top = jnp.maximum(jnp.max(s, axis=1, keepdims=True), s_new)
         e = jnp.exp(s - top)
         e_new = jnp.exp(s_new - top)
-        den = jnp.sum(e, axis=0, keepdims=True) + e_new
-        p = (e / den).T
-        p_new = jnp.broadcast_to((e_new / den).astype(BF).astype(F32), (128, 128)).T
-        row_p = lax.broadcasted_iota(jnp.int32, (128, 256), 0) % 8
-        p_big = jnp.concatenate([jnp.where(row_p == b, p, 0.0).astype(BF) for b in range(8)], axis=1)
-        o = jnp.dot(p_big, cbuf[cs, :, :, pl.ds(0, latent)].reshape(2048, latent), preferred_element_type=F32)
-        kv_rep = jnp.broadcast_to(kv8[None, :, :latent], (16, 8, latent)).reshape(128, latent)
-        o = o + jnp.concatenate([p_new] * (latent // 128), axis=1) * kv_rep
+        den = jnp.sum(e, axis=1, keepdims=True) + e_new
+        p = e / den
+        o = (e_new / den).astype(BF).astype(F32) * kv_rep[:, :latent]
+        for b in range(8):
+            o = o + lax.dot_general(jnp.where(row == b, p, 0.0).astype(BF), cbuf[cs, b, pl.ds(0, latent), :], nt, preferred_element_type=F32)
         part[:, :, :, rows8, pl.ds(1024, latent)] = o.reshape(2, 2, 4, 8, latent)
 
         @pl.when(g + 2 < num_seq // 8)
@@ -267,12 +263,8 @@
             u = jnp.dot(x(), gbuf[uslot, :, pl.ds(start, size)], preferred_element_type=F32)
             store(start, size, (g * jax.nn.sigmoid(g) * u).astype(BF))
 
-        @pl.loop(0, ff // 256)
-        def _(n):
-            block(pl.multiple_of(n * 256, 256), 256)
-
-        if ff % 256:
-            block(ff - ff % 256, ff % 256)
+        for start in range(0, ff, 512):
+            block(start, min(512, ff - start))
 
     def g_wait(k):
         g_copy(k).wait()
@@ -415,7 +407,7 @@
 def layer(x, lens, routes, route_gates, cache, w_q, w_dkv, w_uk, w_uv, w_o, sh_gate, sh_up, sh_down, ex_gate, ex_up, ex_down):
     num_seq, hidden = x.shape
     num_loc, _, ff = ex_gate.shape
-    lat_row = cache.shape[2]
+    lat_row = cache.shape[1]
     ntok = 16 * num_seq
     dma = pltpu.SemaphoreType.DMA
     vm = pl.BlockSpec(memory_space=pltpu.VMEM)
@@ -428,10 +420,11 @@
         scratch_shapes=[
             pltpu.VMEM((NG, hidden, ff), BF),
             pltpu.VMEM((ND, ff, hidden // NCH), BF),
-            pltpu.VMEM((2, 8, cache.shape[1], lat_row), BF),
-            pltpu.VMEM((hidden, lat_row), BF),
+            pltpu.VMEM((2, 8, lat_row, cache.shape[2]), BF),
+            pltpu.VMEM((lat_row, hidden), BF),
             pltpu.VMEM((16, num_seq, 128), BF),
             pltpu.VMEM((num_seq, 640), F32),
+            pltpu.VMEM((num_seq, 128), F32),
             pltpu.VMEM((num_seq, hidden), BF),
             pltpu.VMEM((num_seq, hidden), BF),
             pltpu.VMEM((num_seq, 128), F32),
@@ -459,10 +452,10 @@
 
 def solution(mesh):
     def device_step(x_blk, cache_blk, len_blk, routes, route_gates, w_q, w_dkv, w_uk, w_uv, w_o, sh_gate, sh_up, sh_down, ex_gate, ex_up, ex_down):
-        lens = jnp.broadcast_to(len_blk[:, None], (len_blk.shape[0], 128))
+        lens = len_blk[None, :]
         uk = w_uk.reshape(-1, w_uk.shape[2])
         uv = w_uv.reshape(-1, w_uv.shape[2])
-        return layer(x_blk, lens, routes, route_gates, cache_blk, w_q, w_dkv, uk, uv, w_o, sh_gate, sh_up, sh_down, ex_gate, ex_up, ex_down)
+        return layer(x_blk, lens, routes.T, route_gates.T, cache_blk.transpose(0, 2, 1), w_q, w_dkv.T, uk, uv, w_o, sh_gate, sh_up, sh_down, ex_gate, ex_up, ex_down)
 
     batch_spec = P(("dp", "ep"))
     weight_spec = P()

time: 125 us -> 99.4 us (0.80)
  local copies, waits for them, and re-layouts: 25.8 us -> 2.97 us
  Pallas kernels: 98.2 us -> 95.6 us
    unnamed x6 -> x2, local copies, waits for them, and re-layouts: 24.5 us -> 2.97 us
    pallas_call x1, Pallas kernels: 98.2 us -> 95.6 us  [layer(): pl.pallas_call(layer_kernel, out_shape=(jax.ShapeDtypeStruct((num_seq, hi...]
    broadcast_in_dim x1 -> x0, local copies, waits for them, and re-layouts: 1.33 us -> none  [device_step(): lens = jnp.broadcast_to(len_blk[:, None], (len_blk.shape[0], 128))]
where the time goes in v4:
time: 99.4 us; the launch traced here: 99.2 us
  Pallas kernels  95.6 us (96%)
  local copies, waits for them, and re-layouts  2.97 us (3%)
    pallas_call x1, Pallas kernels, layer(): pl.pallas_call(layer_kernel, out_shape=(jax.ShapeDtypeStruct((num_seq, hi...  95.6 us
    unnamed x2, local copies, waits for them, and re-layouts  2.97 us

profile of v4, /device:TPU:0, one launch (start us, length us, event | category | flops | bytes accessed | tf_op | source)
XLA Modules:
  0.0 99.2 jit_solution(16777193277597922236)
XLA Ops:
  0.6 95.6 %layer.1 = (bf16[32,2048]{1,0:T(8,128)(2,1)}, bf16[32,576]{1,0:T(8,128)(2,1)}) custom-call(bf16[32,2048]{1,0:T(8,128)(2,1)} %x_ref.1, s32[1,32]{1,0:T(1,128)} %bitcast.13, s32[6,32]{1,0:T(8,128)} %bitcast.11, f32[6,32]{1,0:T(8,128)} %bitcast.12, bf16[32,576,256]{2,1,0:T(8,128)(2,1)} %bitcast.7, bf16[2048,3072]{1,0:T(8,128)(2,1)} %wq_ref.1, ...), custom_call_target="tpu_custom_call" | custom-call | tf_op jit(solution)/shard_map/layer/pallas_call | solution.py:415
  96.2 1.6 %copy.20 = bf16[32,2048]{1,0:T(8,128)(2,1)} copy(bf16[32,2048]{1,0:T(8,128)(2,1)} %get-tuple-element.4) | data formatting | bytes 262144
  97.8 1.4 %copy.21 = bf16[32,576]{1,0:T(8,128)(2,1)} copy(bf16[32,576]{1,0:T(8,128)(2,1)} %get-tuple-element.5) | data formatting | bytes 73728

commit v5 on v4

--- a/solution.py
+++ b/solution.py
@@ -14,7 +14,8 @@
 
 NG = 5
 ND = 8
-NCH = 4
+NCH = 8
+NA = 2
 
 
 def layer_kernel(x_ref, len_ref, routes_ref, rgate_ref, cache_ref, wq_ref, wdkv_ref, wuk_ref, wuv_ref, wo_ref,
@@ -23,19 +24,23 @@
                  h_all, meta_all, meta_t, sel, sel_t, gates, xe, act, act_sh, shared,
                  part, rc, ry, rz,
                  gsem, dsem, csem, xsem, ag_send, ag_recv, am_send, am_recv,
-                 s1_send, s1_recv, s2_send, s2_recv, s3_send, s3_recv):
+                 s1_send, s1_recv, s2_send, s2_recv, s3_send, s3_recv, s4_send, s4_recv):
     me = lax.axis_index("ep")
     c = lax.rem(me, 2)
     y = lax.rem(lax.div(me, 2), 2)
     z = lax.div(me, 4)
     core_peer = me + 1 - 2 * c
     y_peer = me + 2 - 4 * y
-    zs = [lax.rem(z + d, 4) for d in range(4)]
-    zback = [lax.rem(z + 4 - d, 4) for d in range(4)]
-    z_peers = [me + 4 * (zs[d] - z) for d in range(4)]
+    za = z + 1 - 2 * lax.rem(z, 2)
+    zb = z + 2 - 4 * lax.div(z, 2)
+    zc = za + zb - z
+    za_peer = me + 4 * (za - z)
+    zb_peer = me + 4 * (zb - z)
     num_loc, hidden, ff = eg_ref.shape
     num_seq = x_ref.shape[0]
     cw = hidden // NCH
+    dw = 2 * cw
+    aw = hidden // NA
     latent = wuk_ref.shape[1]
     num_heads = part.shape[0] * part.shape[1] * part.shape[2]
     nope = wuk_ref.shape[0] // num_heads
@@ -58,10 +63,10 @@
             src, dst = wo_ref.at[:, pl.ds(ff, OB)], gbuf.at[slot, :, pl.ds(0, OB)]
         elif k == 4:
             src = wo_ref.at[:, pl.ds(0, ff)]
-        elif k < 9:
-            src = (su_ref, sg_ref)[k % 2].at[:, pl.ds((k - 5) // 2 * ff, ff)]
+        elif k < 13:
+            src = (eu_ref, eg_ref)[k % 2].at[(k - 5) // 2]
         else:
-            src = (eu_ref, eg_ref)[k % 2].at[(k - 9) // 2]
+            src = (su_ref, sg_ref)[k % 2].at[:, pl.ds((k - 13) // 2 * ff, ff)]
         return pltpu.make_async_copy(src, dst, gsem.at[slot])
 
     def uk_copy():
@@ -78,11 +83,11 @@
 
     def d_copy(p):
         slot = p % ND
-        if p < 8:
-            src = sd_ref.at[pl.ds((p % 2) * ff, ff), pl.ds((p // 2) * cw, cw)]
+        if p < 16:
+            src = ed_ref.at[p % 4, :, pl.ds((p // 4) * dw, dw)]
         else:
-            q = p - 8
-            src = ed_ref.at[q % 4, :, pl.ds((q // 4) * cw, cw)]
+            q = p - 16
+            src = sd_ref.at[pl.ds((q % 2) * ff, ff), pl.ds((q // 2) * dw, dw)]
         return pltpu.make_async_copy(src, dbuf.at[slot], dsem.at[slot])
 
     g_copy(0).start()
@@ -98,7 +103,7 @@
     g_copy(4).start()
 
     barrier = pltpu.get_barrier_semaphore()
-    peers = [core_peer, y_peer, z_peers[1], z_peers[2], z_peers[3]]
+    peers = [core_peer, y_peer, za_peer, zb_peer]
     for peer in peers:
         pl.semaphore_signal(barrier, inc=1, device_id={"ep": peer}, device_id_type=MESH)
 
@@ -128,48 +133,53 @@
         turned = jnp.where(lane < rope // 2, pltpu.roll(v, 128 - rope // 2, 1), pltpu.roll(v, rope // 2, 1))
         return v * cos_w + turned * sin_w
 
-    pl.semaphore_wait(barrier, len(peers))
-
-    def ag(src_pos, peer, n, own, table):
+    def ag(src_pos, peer, n, own, part_no):
         cc, yy, zz = src_pos
         idx = (cc * 2 + yy) * 4 + zz
-        if table:
-            mine_ref, all_ref, ss, rs = meta_own, meta_all, am_send, am_recv
-        else:
-            mine_ref, all_ref, ss, rs = h_own, h_all, ag_send, ag_recv
-        return pltpu.make_async_remote_copy(src_ref=mine_ref if own else all_ref.at[cc, yy, zz], dst_ref=all_ref.at[cc, yy, zz], send_sem=ss.at[n], recv_sem=rs.at[idx], device_id={"ep": peer}, device_id_type=MESH)
+        if part_no is None:
+            src = meta_own if own else meta_all.at[cc, yy, zz]
+            return pltpu.make_async_remote_copy(src_ref=src, dst_ref=meta_all.at[cc, yy, zz], send_sem=am_send.at[n], recv_sem=am_recv.at[idx], device_id={"ep": peer}, device_id_type=MESH)
+        cols = pl.ds(part_no * aw, aw)
+        src = h_own.at[:, cols] if own else h_all.at[cc, yy, zz, :, cols]
+        return pltpu.make_async_remote_copy(src_ref=src, dst_ref=h_all.at[cc, yy, zz, :, cols], send_sem=ag_send.at[part_no * 15 + n], recv_sem=ag_recv.at[part_no * 16 + idx], device_id={"ep": peer}, device_id_type=MESH)
 
     started = []
 
-    def send(src_pos, peer, n, table, own=False):
-        a = ag(src_pos, peer, n, own, table)
+    def send(src_pos, peer, n, part_no, own=False):
+        a = ag(src_pos, peer, n, own, part_no)
         a.start()
         started.append(a)
 
-    def arrive(src_pos, table):
-        ag(src_pos, core_peer, 0, False, table).wait_recv()
-
-    mine = (c, y, z)
-
-    def send_own(table):
-        send(mine, y_peer, 0, table, True)
-        for d in (1, 2, 3):
-            send(mine, z_peers[d], d, table, True)
-        send(mine, core_peer, 4, table, True)
-
-    def fwd_z(d, table=False):
-        pos = (c, y, zback[d])
-        arrive(pos, table)
-        send(pos, y_peer, 4 + d, table)
-        send(pos, core_peer, 7 + d, table)
-
-    def fwd_y(d, table=False):
-        pos = (c, 1 - y, zback[d])
-        arrive(pos, table)
-        send(pos, core_peer, 11 + d, table)
-
-    send_own(True)
-    meta_all[c, y, z] = meta_own[...]
+    def arrive(src_pos, part_no):
+        ag(src_pos, core_peer, 0, False, part_no).wait_recv()
+
+    def send_own(part_no):
+        for n, peer in enumerate((zb_peer, y_peer, za_peer, core_peer)):
+            send((c, y, z), peer, n, part_no, True)
+
+    def fwd_zb(part_no):
+        pos = (c, y, zb)
+        arrive(pos, part_no)
+        send(pos, za_peer, 4, part_no)
+        send(pos, y_peer, 5, part_no)
+        send(pos, core_peer, 6, part_no)
+
+    def fwd_za(part_no):
+        pos = (c, y, za)
+        arrive(pos, part_no)
+        send(pos, y_peer, 7, part_no)
+        send(pos, core_peer, 8, part_no)
+
+    def fwd_zc(part_no):
+        pos = (c, y, zc)
+        arrive(pos, part_no)
+        send(pos, y_peer, 9, part_no)
+        send(pos, core_peer, 10, part_no)
+
+    def fwd_y(i, part_no):
+        pos = (c, 1 - y, (z, zb, za, zc)[i])
+        arrive(pos, part_no)
+        send(pos, core_peer, 11 + i, part_no)
 
     def hidx(h):
         return h // 8, h // 4 % 2, h % 4
@@ -192,8 +202,6 @@
     for h in range(num_heads):
         part[(*hidx(h), slice(None), pl.ds(0, latent))] = jnp.dot(qn[h], gbuf[2, pl.ds(h * nope, nope), pl.ds(W4, latent)], preferred_element_type=F32)
     g_copy(7).start()
-    for d in (1, 2, 3):
-        fwd_z(d, True)
 
     nt = (((1,), (1,)), ((), ()))
     dkv_copy().wait()
@@ -240,63 +248,54 @@
 
     for p in range(ND):
         d_copy(p).start()
-    for d in range(4):
-        fwd_y(d, True)
+    pl.semaphore_wait(barrier, len(peers))
+    send_own(None)
+    meta_all[c, y, z] = meta_own[...]
     for i in range(4):
         uv_copy(i).wait()
     g_copy(3).wait()
     for h in range(num_heads):
         ob = part[(*hidx(h), slice(None), pl.ds(1024, latent))].astype(BF)
         vcat[:, h * 128:(h + 1) * 128] = jnp.dot(ob, gbuf[3, pl.ds(h % 4 * latent, latent), pl.ds(OB + 128 * (h // 4), 128)], preferred_element_type=F32).astype(BF)
+    fwd_zb(None)
+    fwd_za(None)
     g_copy(4).wait()
     for lo, hi, slot in ((0, ff, 4), (ff, hidden, 3)):
         a = jnp.dot(vcat[...], gbuf[slot, :, pl.ds(0, hi - lo)], preferred_element_type=F32).astype(BF)
         h_own[:, lo:hi] = (x_ref[:, lo:hi].astype(F32) + a.astype(F32)).astype(BF)
+        for i in range(NA):
+            if lo < (i + 1) * aw <= hi:
+                send_own(i)
     g_copy(8).start()
     g_copy(9).start()
-    send_own(False)
     h_all[c, y, z] = h_own[...]
-
-    def gate_up(x, gslot, uslot, store):
-        def block(start, size):
+    fwd_zc(None)
+    for i in range(4):
+        fwd_y(i, None)
+    fwd_za(0)
+    fwd_zb(0)
+    fwd_y(0, 0)
+    fwd_za(1)
+    fwd_zb(1)
+    fwd_zc(0)
+    fwd_y(0, 1)
+    fwd_y(2, 0)
+    fwd_y(1, 0)
+    fwd_zc(1)
+
+    def gate_up(x, gslot, uslot, store, starts=None):
+        for start in starts or range(0, ff, 512):
+            size = min(512, ff - start)
             g = jnp.dot(x(), gbuf[gslot, :, pl.ds(start, size)], preferred_element_type=F32)
             u = jnp.dot(x(), gbuf[uslot, :, pl.ds(start, size)], preferred_element_type=F32)
             store(start, size, (g * jax.nn.sigmoid(g) * u).astype(BF))
 
-        for start in range(0, ff, 512):
-            block(start, min(512, ff - start))
-
     def g_wait(k):
         g_copy(k).wait()
 
-    for s in range(2):
-        g_wait(2 * s + 5)
-        g_wait(2 * s + 6)
-
-        def put(start, size, v, s=s):
-            act_sh[s, :, pl.ds(start, size)] = v
-        gate_up(lambda: h_own[...], (2 * s + 5) % NG, (2 * s + 6) % NG, put)
-        g_copy(2 * s + 10).start()
-        g_copy(2 * s + 11).start()
-        if s == 0:
-            fwd_z(1)
-            fwd_y(0)
-        else:
-            fwd_z(2)
-            fwd_z(3)
-    for j in range(NCH):
-        d_copy(2 * j).wait()
-        d_copy(2 * j + 1).wait()
-        o = jnp.dot(act_sh[0], dbuf[2 * j], preferred_element_type=F32) + jnp.dot(act_sh[1], dbuf[2 * j + 1], preferred_element_type=F32)
-        shared[:, j * cw:(j + 1) * cw] = o.astype(BF)
-        d_copy(2 * j + 8).start()
-        d_copy(2 * j + 9).start()
-        if j >= 1:
-            fwd_y(j)
     for yy in range(2):
         for zz in range(4):
-            arrive((1 - c, yy, zz), True)
-            arrive((1 - c, yy, zz), False)
+            arrive((1 - c, yy, zz), None)
 
     ntok = 16 * num_seq
     rows = 16 * 8
@@ -315,6 +314,15 @@
         code_t = meta_t[pl.ds(ge, 1), :].astype(jnp.int32) + base_row
         sel_t[pl.ds(e * rows, rows), :] = jnp.where(slot_row == code_t, 1.0, 0.0).astype(BF)
 
+    fwd_y(2, 1)
+    fwd_y(1, 1)
+    fwd_y(3, 0)
+    fwd_y(3, 1)
+    for i in range(NA):
+        for yy in range(2):
+            for zz in range(4):
+                arrive((1 - c, yy, zz), i)
+
     @pl.loop(0, hidden // 512)
     def _(n):
         cols = pl.ds(pl.multiple_of(n * 512, 512), 512)
@@ -322,86 +330,124 @@
         xe[:, cols] = jnp.dot(sel_t[...], hh, preferred_element_type=F32).astype(BF)
 
     for e in range(num_loc):
-        g_wait(9 + 2 * e)
-        g_wait(10 + 2 * e)
+        g_wait(5 + 2 * e)
+        g_wait(6 + 2 * e)
 
         def put(start, size, v, e=e):
             act[e, :, pl.ds(start, size)] = v
-        gate_up(lambda e=e: xe[pl.ds(e * rows, rows), :], (9 + 2 * e) % NG, (10 + 2 * e) % NG, put)
-        for k in (14 + 2 * e, 15 + 2 * e):
-            if k < 9 + 2 * num_loc:
+        gate_up(lambda e=e: xe[pl.ds(e * rows, rows), :], (5 + 2 * e) % NG, (6 + 2 * e) % NG, put)
+        for k in (10 + 2 * e, 11 + 2 * e):
+            if k < 17:
                 g_copy(k).start()
 
+    def rdma(src, dst, send_sem, recv_sem, peer):
+        return pltpu.make_async_remote_copy(src_ref=src, dst_ref=dst, send_sem=send_sem, recv_sem=recv_sem, device_id={"ep": peer}, device_id_type=MESH)
+
+    def chunk(j):
+        return pl.ds(j * cw, cw)
+
     def s1(j):
-        cols = pl.ds(j * cw, cw)
-        return pltpu.make_async_remote_copy(src_ref=part.at[1 - c, :, :, :, cols], dst_ref=rc.at[:, :, :, cols], send_sem=s1_send.at[j], recv_sem=s1_recv.at[j], device_id={"ep": core_peer}, device_id_type=MESH)
+        return rdma(part.at[1 - c, :, :, :, chunk(j)], rc.at[:, :, :, chunk(j)], s1_send.at[j], s1_recv.at[j], core_peer)
 
     def s2(j):
-        cols = pl.ds(j * cw, cw)
-        return pltpu.make_async_remote_copy(src_ref=part.at[c, 1 - y, :, :, cols], dst_ref=ry.at[:, :, cols], send_sem=s2_send.at[j], recv_sem=s2_recv.at[j], device_id={"ep": y_peer}, device_id_type=MESH)
-
-    def s3(j, d):
-        cols = pl.ds(j * cw, cw)
-        return pltpu.make_async_remote_copy(src_ref=part.at[c, y, zs[d], :, cols], dst_ref=rz.at[d - 1, :, cols], send_sem=s3_send.at[j * 3 + d - 1], recv_sem=s3_recv.at[j * 3 + d - 1], device_id={"ep": z_peers[d]}, device_id_type=MESH)
-
-    def after_s1(j):
-        cols = slice(j * cw, (j + 1) * cw)
+        return rdma(part.at[c, 1 - y, :, :, chunk(j)], ry.at[:, :, chunk(j)], s2_send.at[j], s2_recv.at[j], y_peer)
+
+    def s3(j, i):
+        return rdma(part.at[c, y, (zc, za)[i], :, chunk(j)], rz.at[i, :, chunk(j)], s3_send.at[2 * j + i], s3_recv.at[2 * j + i], za_peer)
+
+    def s4(j):
+        return rdma(part.at[c, y, zb, :, chunk(j)], rz.at[2, :, chunk(j)], s4_send.at[j], s4_recv.at[j], zb_peer)
+
+    def step_a(j):
+        cols = chunk(j)
         s1(j).wait_recv()
         part[c, 1 - y, :, :, cols] = part[c, 1 - y, :, :, cols] + rc[1 - y, :, :, cols]
         s2(j).start()
         part[c, y, :, :, cols] = part[c, y, :, :, cols] + rc[y, :, :, cols]
 
-    def after_s2(j):
-        cols = slice(j * cw, (j + 1) * cw)
+    def step_b(j):
+        cols = chunk(j)
         s2(j).wait_recv()
         part[c, y, :, :, cols] = part[c, y, :, :, cols] + ry[:, :, cols]
-        for d in (2, 1, 3):
-            s3(j, d).start()
+        s3(j, 0).start()
+        s3(j, 1).start()
+
+    def step_c(j):
+        cols = chunk(j)
+        s3(j, 0).wait_recv()
+        part[c, y, zb, :, cols] = part[c, y, zb, :, cols] + rz[0, :, cols]
+        s4(j).start()
+
+    def step_f(j):
+        cols = chunk(j)
+        s3(j, 1).wait_recv()
+        s4(j).wait_recv()
+        routed = part[c, y, z, :, cols] + rz[1, :, cols] + rz[2, :, cols]
+        out_ref[:, cols] = (h_own[:, cols].astype(F32) + shared[:, cols].astype(F32) + routed).astype(BF)
 
     def down(j):
-        cols = pl.ds(j * cw, cw)
+        cols = chunk(j)
+        if j % 2 == 0:
+            for e in range(num_loc):
+                d_copy(2 * j + e).wait()
         for e in range(num_loc):
-            p = 8 + 4 * j + e
-            d_copy(p).wait()
-        for e in range(num_loc):
-            p = 8 + 4 * j + e
-            o = jnp.dot(act[e], dbuf[p % ND], preferred_element_type=F32).astype(BF)
-            if p + ND < 8 + 4 * NCH:
-                d_copy(p + ND).start()
-            for g in range(4):
-                tok = pl.ds(g * ntok // 4, ntok // 4)
-                b = jnp.dot(sel[e, tok, :], o, preferred_element_type=F32)
-                gt = gates[e, tok, :]
-                b = b * jnp.concatenate([gt] * (cw // 128), axis=1)
-                b = b.reshape(4, num_seq, cw)
-                if e == 0:
-                    part[g // 2, g % 2, :, :, cols] = b
-                else:
-                    part[g // 2, g % 2, :, :, cols] = part[g // 2, g % 2, :, :, cols] + b
+            slot = (j // 2 * 4 + e) % ND
+            o = jnp.dot(act[e], dbuf[slot, :, pl.ds(j % 2 * cw, cw)], preferred_element_type=F32).astype(BF)
+            b = jnp.dot(sel[e], o, preferred_element_type=F32)
+            gt = gates[e]
+            b = (b * jnp.concatenate([gt] * (cw // 128), axis=1)).reshape(2, 2, 4, num_seq, cw)
+            if e == 0:
+                part[:, :, :, :, cols] = b
+            else:
+                part[:, :, :, :, cols] = part[:, :, :, :, cols] + b
+        if j % 2 == 1:
+            for e in range(num_loc):
+                d_copy(2 * (j - 1) + 8 + e).start()
+
+    def shared_up(i):
+        s, b = i // 3, i % 3
+        if b == 0:
+            g_wait(13 + 2 * s)
+            g_wait(14 + 2 * s)
+
+        def put(start, size, v):
+            act_sh[s, :, pl.ds(start, size)] = v
+        gate_up(lambda: h_own[...], (13 + 2 * s) % NG, (14 + 2 * s) % NG, put, (512 * b,))
+
+    def shared_down(i):
+        d_copy(16 + 2 * i).wait()
+        d_copy(17 + 2 * i).wait()
+        o = jnp.dot(act_sh[0], dbuf[2 * i], preferred_element_type=F32) + jnp.dot(act_sh[1], dbuf[2 * i + 1], preferred_element_type=F32)
+        shared[:, i * dw:(i + 1) * dw] = o.astype(BF)
 
     for j in range(NCH):
         down(j)
         s1(j).start()
         if j >= 1:
-            after_s1(j - 1)
-        if j >= 2:
-            after_s2(j - 2)
-    after_s1(NCH - 1)
-    after_s2(NCH - 2)
-    after_s2(NCH - 1)
-    for j in range(NCH):
-        cols = slice(j * cw, (j + 1) * cw)
-        for d in (1, 2, 3):
-            s3(j, d).wait_recv()
-        routed = part[c, y, z, :, cols] + rz[0, :, cols] + rz[1, :, cols] + rz[2, :, cols]
-        out_ref[:, cols] = (h_own[:, cols].astype(F32) + shared[:, cols].astype(F32) + routed).astype(BF)
+            step_a(j - 1)
+        if j == 6:
+            step_b(0)
+    step_a(NCH - 1)
+    fill = [lambda i=i: shared_up(i) for i in range(6)] + [lambda i=i: shared_down(i) for i in range(4)]
+    plan = [1, 2, 2, 2, 1, 1, 1]
+    for j in range(1, NCH):
+        step_b(j)
+        for _ in range(plan[j - 1]):
+            fill.pop(0)()
+        step_c(j - 1)
+        if j == NCH - 1:
+            for i in range(NCH - 1):
+                step_f(i)
+    step_c(NCH - 1)
+    step_f(NCH - 1)
     for a in started:
         a.wait_send()
     for j in range(NCH):
         s1(j).wait_send()
         s2(j).wait_send()
-        for d in (1, 2, 3):
-            s3(j, d).wait_send()
+        s3(j, 0).wait_send()
+        s3(j, 1).wait_send()
+        s4(j).wait_send()
 
 
 def layer(x, lens, routes, route_gates, cache, w_q, w_dkv, w_uk, w_uv, w_o, sh_gate, sh_up, sh_down, ex_gate, ex_up, ex_down):
@@ -419,7 +465,7 @@
         out_specs=(vm, vm),
         scratch_shapes=[
             pltpu.VMEM((NG, hidden, ff), BF),
-            pltpu.VMEM((ND, ff, hidden // NCH), BF),
+            pltpu.VMEM((ND, ff, 2 * hidden // NCH), BF),
             pltpu.VMEM((2, 8, lat_row, cache.shape[2]), BF),
             pltpu.VMEM((lat_row, hidden), BF),
             pltpu.VMEM((16, num_seq, 128), BF),
@@ -442,8 +488,8 @@
             pltpu.VMEM((2, 4, num_seq, hidden), F32),
             pltpu.VMEM((4, num_seq, hidden), F32),
             pltpu.VMEM((3, num_seq, hidden), F32),
-            dma((NG,)), dma((ND,)), dma((2,)), dma((6,)), dma((15,)), dma((16,)), dma((15,)), dma((16,)),
-            dma((NCH,)), dma((NCH,)), dma((NCH,)), dma((NCH,)), dma((3 * NCH,)), dma((3 * NCH,)),
+            dma((NG,)), dma((ND,)), dma((2,)), dma((6,)), dma((15 * NA,)), dma((16 * NA,)), dma((15,)), dma((16,)),
+            dma((NCH,)), dma((NCH,)), dma((NCH,)), dma((NCH,)), dma((2 * NCH,)), dma((2 * NCH,)), dma((NCH,)), dma((NCH,)),
         ],
         compiler_params=pltpu.CompilerParams(collective_id=0, has_side_effects=True, vmem_limit_bytes=67043328),
         name="layer",

time: 99.4 us -> 100 us (level)
  no operation moved by 1% of the time
where the time goes in v5:
time: 100 us; the launch traced here: 99.8 us
  Pallas kernels  96.2 us (96%)
  local copies, waits for them, and re-layouts  2.97 us (3%)
    pallas_call x1, Pallas kernels, layer(): pl.pallas_call(layer_kernel, out_shape=(jax.ShapeDtypeStruct((num_seq, hi...  96.2 us
    unnamed x2, local copies, waits for them, and re-layouts  2.97 us

profile of v5, /device:TPU:0, one launch (start us, length us, event | category | flops | bytes accessed | tf_op | source)
XLA Modules:
  0.0 99.8 jit_solution(1150484468226825949)
XLA Ops:
  0.6 96.2 %layer.1 = (bf16[32,2048]{1,0:T(8,128)(2,1)}, bf16[32,576]{1,0:T(8,128)(2,1)}) custom-call(bf16[32,2048]{1,0:T(8,128)(2,1)} %x_ref.1, s32[1,32]{1,0:T(1,128)} %bitcast.13, s32[6,32]{1,0:T(8,128)} %bitcast.11, f32[6,32]{1,0:T(8,128)} %bitcast.12, bf16[32,576,256]{2,1,0:T(8,128)(2,1)} %bitcast.7, bf16[2048,3072]{1,0:T(8,128)(2,1)} %wq_ref.1, ...), custom_call_target="tpu_custom_call" | custom-call | tf_op jit(solution)/shard_map/layer/pallas_call | solution.py:461
  96.8 1.6 %copy.20 = bf16[32,2048]{1,0:T(8,128)(2,1)} copy(bf16[32,2048]{1,0:T(8,128)(2,1)} %get-tuple-element.4) | data formatting | bytes 262144
  98.4 1.4 %copy.21 = bf16[32,576]{1,0:T(8,128)(2,1)} copy(bf16[32,576]{1,0:T(8,128)(2,1)} %get-tuple-element.5) | data formatting | bytes 73728

commit v6 on v5

--- a/solution.py
+++ b/solution.py
@@ -12,7 +12,7 @@
 F32 = jnp.float32
 
 
-NG = 5
+NG = 6
 ND = 8
 NCH = 8
 NA = 2
@@ -20,7 +20,7 @@
 
 def layer_kernel(x_ref, len_ref, routes_ref, rgate_ref, cache_ref, wq_ref, wdkv_ref, wuk_ref, wuv_ref, wo_ref,
                  sg_ref, su_ref, sd_ref, eg_ref, eu_ref, ed_ref, out_ref, kv_ref,
-                 gbuf, dbuf, cbuf, dkv_buf, qn, kvf, lenb, vcat, h_own, meta_own,
+                 gbuf, dbuf, qn, kvf, lenb, vcat, h_own, meta_own,
                  h_all, meta_all, meta_t, sel, sel_t, gates, xe, act, act_sh, shared,
                  part, rc, ry, rz,
                  gsem, dsem, csem, xsem, ag_send, ag_recv, am_send, am_recv,
@@ -47,27 +47,32 @@
     rope = wdkv_ref.shape[0] - latent
     qw = nope + rope
     top_k = routes_ref.shape[0]
+    lat_row, cache_len = cache_ref.shape[1:]
 
     W6 = 6 * qw
     W4 = 4 * qw
     OB = hidden - ff
 
-    def g_copy(k):
-        slot = k % NG
-        dst = gbuf.at[slot]
+    def a_copy(k):
         if k < 2:
-            src, dst = wq_ref.at[:, pl.ds(k * W6, W6)], gbuf.at[slot, :, pl.ds(0, W6)]
+            src, dst = wq_ref.at[:, pl.ds(k * W6, W6)], gbuf.at[k, :, pl.ds(0, W6)]
         elif k == 2:
-            src, dst = wq_ref.at[:, pl.ds(2 * W6, W4)], gbuf.at[slot, :, pl.ds(0, W4)]
+            src, dst = wq_ref.at[:, pl.ds(2 * W6, W4)], gbuf.at[k, :, pl.ds(0, W4)]
         elif k == 3:
-            src, dst = wo_ref.at[:, pl.ds(ff, OB)], gbuf.at[slot, :, pl.ds(0, OB)]
-        elif k == 4:
-            src = wo_ref.at[:, pl.ds(0, ff)]
-        elif k < 13:
-            src = (eu_ref, eg_ref)[k % 2].at[(k - 5) // 2]
+            src, dst = wo_ref.at[:, pl.ds(ff, OB)], gbuf.at[k, :, pl.ds(0, OB)]
         else:
-            src = (su_ref, sg_ref)[k % 2].at[:, pl.ds((k - 13) // 2 * ff, ff)]
-        return pltpu.make_async_copy(src, dst, gsem.at[slot])
+            src, dst = wo_ref.at[:, pl.ds(0, ff)], gbuf.at[k]
+        return pltpu.make_async_copy(src, dst, gsem.at[k])
+
+    def g_slot(m):
+        return m % NG if m < 8 else m - 8
+
+    def g_copy(m):
+        if m < 8:
+            src = (eg_ref, eu_ref)[m % 2].at[m // 2]
+        else:
+            src = (sg_ref, su_ref)[m % 2].at[:, pl.ds((m - 8) // 2 * ff, ff)]
+        return pltpu.make_async_copy(src, gbuf.at[g_slot(m)], gsem.at[g_slot(m)])
 
     def uk_copy():
         return pltpu.make_async_copy(wuk_ref, gbuf.at[2, :, pl.ds(W4, latent)], xsem.at[0])
@@ -75,32 +80,41 @@
     def uv_copy(i):
         return pltpu.make_async_copy(wuv_ref.at[pl.ds(i * hidden, hidden)], gbuf.at[3, :, pl.ds(OB + 128 * i, 128)], xsem.at[1 + i])
 
-    def dkv_copy():
-        return pltpu.make_async_copy(wdkv_ref, dkv_buf, xsem.at[5])
-
-    def c_copy(g, slot):
-        return pltpu.make_async_copy(cache_ref.at[pl.ds(g * 8, 8)], cbuf.at[slot], csem.at[slot])
+    def dkv_copy(i):
+        lo, size = ((0, ff), (ff, OB))[i]
+        return pltpu.make_async_copy(wdkv_ref.at[:, pl.ds(lo, size)], gbuf.at[5, pl.ds(i * lat_row, lat_row), pl.ds(0, size)], xsem.at[5 + i])
+
+    def cache_at(i, slot):
+        return slot, pl.ds(i % 4 // 2 * lat_row, lat_row), pl.ds(i % 2 * cache_len, cache_len)
+
+    def c_copy(i, seq, slot):
+        return pltpu.make_async_copy(cache_ref.at[seq], dbuf.at[cache_at(i, slot)], csem.at[seq])
+
+    def d_place(p):
+        if 8 <= p < 16:
+            return gbuf, (2 + (p - 8) // 2, pl.ds(0, ff), pl.ds(p % 2 * dw, dw))
+        return dbuf, (p % ND, slice(None), slice(None))
 
     def d_copy(p):
-        slot = p % ND
         if p < 16:
             src = ed_ref.at[p % 4, :, pl.ds((p // 4) * dw, dw)]
         else:
             q = p - 16
             src = sd_ref.at[pl.ds((q % 2) * ff, ff), pl.ds((q // 2) * dw, dw)]
-        return pltpu.make_async_copy(src, dbuf.at[slot], dsem.at[slot])
-
-    g_copy(0).start()
-    g_copy(1).start()
-    g_copy(2).start()
+        buf, at = d_place(p)
+        return pltpu.make_async_copy(src, buf.at[at], dsem.at[p % 16])
+
+    for k in range(3):
+        a_copy(k).start()
     uk_copy().start()
-    dkv_copy().start()
-    c_copy(0, 0).start()
-    c_copy(1, 1).start()
-    g_copy(3).start()
+    dkv_copy(0).start()
+    dkv_copy(1).start()
+    for i in range(num_seq):
+        c_copy(i, i, i // 4).start()
+    a_copy(3).start()
     for i in range(4):
         uv_copy(i).start()
-    g_copy(4).start()
+    a_copy(4).start()
 
     barrier = pltpu.get_barrier_semaphore()
     peers = [core_peer, y_peer, za_peer, zb_peer]
@@ -185,7 +199,7 @@
         return h // 8, h // 4 % 2, h % 4
 
     def q_heads(k, first, count):
-        g_copy(k).wait()
+        a_copy(k).wait()
         qq = jnp.dot(x_ref[...], gbuf[k, :, pl.ds(0, count * qw)], preferred_element_type=F32).astype(BF).astype(F32)
         for i in range(count // 2):
             pair = qq[:, 2 * i * qw:2 * (i + 1) * qw]
@@ -194,18 +208,23 @@
                 part[(*hidx(h), slice(None), pl.ds(latent, 128))] = rotate(v[:, nope:nope + 128])
 
     q_heads(0, 0, 6)
-    g_copy(5).start()
+    g_copy(0).start()
     q_heads(1, 6, 6)
-    g_copy(6).start()
+    g_copy(1).start()
     q_heads(2, 12, 4)
     uk_copy().wait()
     for h in range(num_heads):
         part[(*hidx(h), slice(None), pl.ds(0, latent))] = jnp.dot(qn[h], gbuf[2, pl.ds(h * nope, nope), pl.ds(W4, latent)], preferred_element_type=F32)
-    g_copy(7).start()
+    g_copy(2).start()
+    pl.semaphore_wait(barrier, len(peers))
+    send_own(None)
+    meta_all[c, y, z] = meta_own[...]
 
     nt = (((1,), (1,)), ((), ()))
-    dkv_copy().wait()
-    r = lax.dot_general(x_ref[...], dkv_buf[...], nt, preferred_element_type=F32)
+    dkv_copy(0).wait()
+    dkv_copy(1).wait()
+    r = lax.dot_general(x_ref[:, :ff], gbuf[5, pl.ds(0, lat_row), :], nt, preferred_element_type=F32) + lax.dot_general(x_ref[:, ff:], gbuf[5, pl.ds(lat_row, lat_row), pl.ds(0, OB)], nt, preferred_element_type=F32)
+    g_copy(5).start()
     r_lat = r[:, :latent].astype(BF)
     r_rope = rotate(jnp.concatenate([r[:, latent:], jnp.zeros((num_seq, 128 - rope), F32)], axis=1)).astype(BF)
     kvf[:, :latent] = r_lat.astype(F32)
@@ -217,8 +236,8 @@
 
     @pl.loop(0, num_seq // 8)
     def _(g):
-        cs = lax.rem(g, 2)
-        c_copy(g, cs).wait()
+        for b in range(8):
+            c_copy(b, g * 8 + b, 2 * g + b // 4).wait()
         rows8 = pl.ds(pl.multiple_of(g * 8, 8), 8)
         q = part[:, :, :, rows8, pl.ds(0, latent + 128)].reshape(128, latent + 128).astype(BF)
         kv_rep = jnp.broadcast_to(kvf[rows8, :][None], (16, 8, latent + 128)).reshape(128, latent + 128)
@@ -230,7 +249,7 @@
         q = q[:, :latent + rope]
         s = jnp.zeros((128, 256), F32)
         for b in range(8):
-            s = jnp.where(row == b, jnp.dot(q, cbuf[cs, b], preferred_element_type=F32), s)
+            s = jnp.where(row == b, jnp.dot(q, dbuf[cache_at(b, 2 * g + b // 4)], preferred_element_type=F32), s)
         s = jnp.where(pos < n_rep, s * scale, -jnp.inf)
         top = jnp.maximum(jnp.max(s, axis=1, keepdims=True), s_new)
         e = jnp.exp(s - top)
@@ -239,37 +258,30 @@
         p = e / den
         o = (e_new / den).astype(BF).astype(F32) * kv_rep[:, :latent]
         for b in range(8):
-            o = o + lax.dot_general(jnp.where(row == b, p, 0.0).astype(BF), cbuf[cs, b, pl.ds(0, latent), :], nt, preferred_element_type=F32)
+            o = o + lax.dot_general(jnp.where(row == b, p, 0.0).astype(BF), dbuf[cache_at(b, 2 * g + b // 4)][:latent], nt, preferred_element_type=F32)
         part[:, :, :, rows8, pl.ds(1024, latent)] = o.reshape(2, 2, 4, 8, latent)
-
-        @pl.when(g + 2 < num_seq // 8)
-        def _():
-            c_copy(g + 2, cs).start()
 
     for p in range(ND):
         d_copy(p).start()
-    pl.semaphore_wait(barrier, len(peers))
-    send_own(None)
-    meta_all[c, y, z] = meta_own[...]
+    fwd_zb(None)
+    fwd_za(None)
     for i in range(4):
         uv_copy(i).wait()
-    g_copy(3).wait()
+    a_copy(3).wait()
     for h in range(num_heads):
         ob = part[(*hidx(h), slice(None), pl.ds(1024, latent))].astype(BF)
         vcat[:, h * 128:(h + 1) * 128] = jnp.dot(ob, gbuf[3, pl.ds(h % 4 * latent, latent), pl.ds(OB + 128 * (h // 4), 128)], preferred_element_type=F32).astype(BF)
-    fwd_zb(None)
-    fwd_za(None)
-    g_copy(4).wait()
+    a_copy(4).wait()
+    fwd_zc(None)
     for lo, hi, slot in ((0, ff, 4), (ff, hidden, 3)):
         a = jnp.dot(vcat[...], gbuf[slot, :, pl.ds(0, hi - lo)], preferred_element_type=F32).astype(BF)
         h_own[:, lo:hi] = (x_ref[:, lo:hi].astype(F32) + a.astype(F32)).astype(BF)
         for i in range(NA):
             if lo < (i + 1) * aw <= hi:
                 send_own(i)
-    g_copy(8).start()
-    g_copy(9).start()
+    g_copy(3).start()
+    g_copy(4).start()
     h_all[c, y, z] = h_own[...]
-    fwd_zc(None)
     for i in range(4):
         fwd_y(i, None)
     fwd_za(0)
@@ -330,15 +342,21 @@
         xe[:, cols] = jnp.dot(sel_t[...], hh, preferred_element_type=F32).astype(BF)
 
     for e in range(num_loc):
-        g_wait(5 + 2 * e)
-        g_wait(6 + 2 * e)
+        g_wait(2 * e)
+        g_wait(2 * e + 1)
 
         def put(start, size, v, e=e):
             act[e, :, pl.ds(start, size)] = v
-        gate_up(lambda e=e: xe[pl.ds(e * rows, rows), :], (5 + 2 * e) % NG, (6 + 2 * e) % NG, put)
-        for k in (10 + 2 * e, 11 + 2 * e):
-            if k < 17:
-                g_copy(k).start()
+        gate_up(lambda e=e: xe[pl.ds(e * rows, rows), :], g_slot(2 * e), g_slot(2 * e + 1), put)
+        if e == 0:
+            g_copy(6).start()
+            g_copy(7).start()
+        elif e < 3:
+            for p in range(4 * e + 4, 4 * e + 8):
+                d_copy(p).start()
+        else:
+            g_copy(8).start()
+            g_copy(9).start()
 
     def rdma(src, dst, send_sem, recv_sem, peer):
         return pltpu.make_async_remote_copy(src_ref=src, dst_ref=dst, send_sem=send_sem, recv_sem=recv_sem, device_id={"ep": peer}, device_id_type=MESH)
@@ -391,8 +409,8 @@
             for e in range(num_loc):
                 d_copy(2 * j + e).wait()
         for e in range(num_loc):
-            slot = (j // 2 * 4 + e) % ND
-            o = jnp.dot(act[e], dbuf[slot, :, pl.ds(j % 2 * cw, cw)], preferred_element_type=F32).astype(BF)
+            buf, at = d_place(j // 2 * 4 + e)
+            o = jnp.dot(act[e], buf[at[0], at[1], pl.ds(j % 2 * cw + (j // 2 > 1) * (e % 2) * dw, cw)] if buf is gbuf else buf[at[0], :, pl.ds(j % 2 * cw, cw)], preferred_element_type=F32).astype(BF)
             b = jnp.dot(sel[e], o, preferred_element_type=F32)
             gt = gates[e]
             b = (b * jnp.concatenate([gt] * (cw // 128), axis=1)).reshape(2, 2, 4, num_seq, cw)
@@ -400,19 +418,22 @@
                 part[:, :, :, :, cols] = b
             else:
                 part[:, :, :, :, cols] = part[:, :, :, :, cols] + b
-        if j % 2 == 1:
+        if j in (1, 3):
             for e in range(num_loc):
-                d_copy(2 * (j - 1) + 8 + e).start()
+                d_copy(16 + 2 * (j - 1) + e).start()
+        if j == 5:
+            g_copy(10).start()
+            g_copy(11).start()
 
     def shared_up(i):
         s, b = i // 3, i % 3
         if b == 0:
-            g_wait(13 + 2 * s)
-            g_wait(14 + 2 * s)
+            g_wait(8 + 2 * s)
+            g_wait(9 + 2 * s)
 
         def put(start, size, v):
             act_sh[s, :, pl.ds(start, size)] = v
-        gate_up(lambda: h_own[...], (13 + 2 * s) % NG, (14 + 2 * s) % NG, put, (512 * b,))
+        gate_up(lambda: h_own[...], g_slot(8 + 2 * s), g_slot(9 + 2 * s), put, (512 * b,))
 
     def shared_down(i):
         d_copy(16 + 2 * i).wait()
@@ -466,8 +487,6 @@
         scratch_shapes=[
             pltpu.VMEM((NG, hidden, ff), BF),
             pltpu.VMEM((ND, ff, 2 * hidden // NCH), BF),
-            pltpu.VMEM((2, 8, lat_row, cache.shape[2]), BF),
-            pltpu.VMEM((lat_row, hidden), BF),
             pltpu.VMEM((16, num_seq, 128), BF),
             pltpu.VMEM((num_seq, 640), F32),
             pltpu.VMEM((num_seq, 128), F32),
@@ -488,7 +507,7 @@
             pltpu.VMEM((2, 4, num_seq, hidden), F32),
             pltpu.VMEM((4, num_seq, hidden), F32),
             pltpu.VMEM((3, num_seq, hidden), F32),
-            dma((NG,)), dma((ND,)), dma((2,)), dma((6,)), dma((15 * NA,)), dma((16 * NA,)), dma((15,)), dma((16,)),
+            dma((NG,)), dma((16,)), dma((num_seq,)), dma((7,)), dma((15 * NA,)), dma((16 * NA,)), dma((15,)), dma((16,)),
             dma((NCH,)), dma((NCH,)), dma((NCH,)), dma((NCH,)), dma((2 * NCH,)), dma((2 * NCH,)), dma((NCH,)), dma((NCH,)),
         ],
         compiler_params=pltpu.CompilerParams(collective_id=0, has_side_effects=True, vmem_limit_bytes=67043328),

time: 100 us -> 93 us (0.930)
  Pallas kernels: 96.2 us -> 89.2 us
    pallas_call x1, Pallas kernels: 96.2 us -> 89.2 us  [layer(): pl.pallas_call(layer_kernel, out_shape=(jax.ShapeDtypeStruct((num_seq, hi...]
where the time goes in v6:
time: 93 us; the launch traced here: 92.8 us
  Pallas kernels  89.2 us (96%)
  local copies, waits for them, and re-layouts  2.97 us (3%)
    pallas_call x1, Pallas kernels, layer(): pl.pallas_call(layer_kernel, out_shape=(jax.ShapeDtypeStruct((num_seq, hi...  89.2 us
    unnamed x2, local copies, waits for them, and re-layouts  2.97 us

profile of v6, /device:TPU:0, one launch (start us, length us, event | category | flops | bytes accessed | tf_op | source)
XLA Modules:
  0.0 92.8 jit_solution(11958388242586915378)
XLA Ops:
  0.6 89.2 %layer.1 = (bf16[32,2048]{1,0:T(8,128)(2,1)}, bf16[32,576]{1,0:T(8,128)(2,1)}) custom-call(bf16[32,2048]{1,0:T(8,128)(2,1)} %x_ref.1, s32[1,32]{1,0:T(1,128)} %bitcast.13, s32[6,32]{1,0:T(8,128)} %bitcast.11, f32[6,32]{1,0:T(8,128)} %bitcast.12, bf16[32,576,256]{2,1,0:T(8,128)(2,1)} %bitcast.7, bf16[2048,3072]{1,0:T(8,128)(2,1)} %wq_ref.1, ...), custom_call_target="tpu_custom_call" | custom-call | tf_op jit(solution)/shard_map/layer/pallas_call | solution.py:482
  89.8 1.6 %copy.20 = bf16[32,2048]{1,0:T(8,128)(2,1)} copy(bf16[32,2048]{1,0:T(8,128)(2,1)} %get-tuple-element.4) | data formatting | bytes 262144
  91.4 1.4 %copy.21 = bf16[32,576]{1,0:T(8,128)(2,1)} copy(bf16[32,576]{1,0:T(8,128)(2,1)} %get-tuple-element.5) | data formatting | bytes 73728

commit v7 on v6

--- a/solution.py
+++ b/solution.py
@@ -12,10 +12,13 @@
 F32 = jnp.float32
 
 
+LN = 128
 NG = 6
 ND = 8
 NCH = 8
 NA = 2
+ZYC = (2, 2, 4)
+YLAST = (0, 2)
 
 
 def layer_kernel(x_ref, len_ref, routes_ref, rgate_ref, cache_ref, wq_ref, wdkv_ref, wuk_ref, wuv_ref, wo_ref,
@@ -78,7 +81,7 @@
         return pltpu.make_async_copy(wuk_ref, gbuf.at[2, :, pl.ds(W4, latent)], xsem.at[0])
 
     def uv_copy(i):
-        return pltpu.make_async_copy(wuv_ref.at[pl.ds(i * hidden, hidden)], gbuf.at[3, :, pl.ds(OB + 128 * i, 128)], xsem.at[1 + i])
+        return pltpu.make_async_copy(wuv_ref.at[pl.ds(i * hidden, hidden)], gbuf.at[3, :, pl.ds(OB + LN * i, LN)], xsem.at[1 + i])
 
     def dkv_copy(i):
         lo, size = ((0, ff), (ff, OB))[i]
@@ -121,14 +124,14 @@
     for peer in peers:
         pl.semaphore_signal(barrier, inc=1, device_id={"ep": peer}, device_id_type=MESH)
 
-    lane = lax.broadcasted_iota(jnp.int32, (num_seq, 128), 1)
+    lane = lax.broadcasted_iota(jnp.int32, (num_seq, LN), 1)
     pad_k = jnp.zeros((8 - top_k, num_seq), F32)
     small = jnp.concatenate([routes_ref[...].astype(F32), pad_k, rgate_ref[...], pad_k, len_ref[...].astype(F32), jnp.zeros((15, num_seq), F32)], axis=0)
-    small = jnp.concatenate([small, jnp.zeros((32, 128 - num_seq), F32)], axis=1)
-    cols = jnp.concatenate([small, jnp.zeros((96, 128), F32)], axis=0).T[:num_seq]
-    lenb[...] = jnp.broadcast_to(cols[:, 16:17], (num_seq, 128))
-    member = jnp.zeros((num_seq, 128), F32)
-    gate_te = jnp.zeros((num_seq, 128), F32)
+    small = jnp.concatenate([small, jnp.zeros((32, LN - num_seq), F32)], axis=1)
+    cols = jnp.concatenate([small, jnp.zeros((96, LN), F32)], axis=0).T[:num_seq]
+    lenb[...] = jnp.broadcast_to(cols[:, 16:17], (num_seq, LN))
+    member = jnp.zeros((num_seq, LN), F32)
+    gate_te = jnp.zeros((num_seq, LN), F32)
     for k in range(top_k):
         hit = (lane % 64).astype(F32) == cols[:, k:k + 1]
         member = jnp.where(hit, 1.0, member)
@@ -144,7 +147,7 @@
     sin_w = jnp.where(live, jnp.where(lane < rope // 2, -jnp.sin(angle), jnp.sin(angle)), 0.0)
 
     def rotate(v):
-        turned = jnp.where(lane < rope // 2, pltpu.roll(v, 128 - rope // 2, 1), pltpu.roll(v, rope // 2, 1))
+        turned = jnp.where(lane < rope // 2, pltpu.roll(v, LN - rope // 2, 1), pltpu.roll(v, rope // 2, 1))
         return v * cos_w + turned * sin_w
 
     def ag(src_pos, peer, n, own, part_no):
@@ -205,7 +208,7 @@
             pair = qq[:, 2 * i * qw:2 * (i + 1) * qw]
             for h, v in ((first + 2 * i, pair), (first + 2 * i + 1, pltpu.roll(pair, qw, 1))):
                 qn[h] = v[:, :nope].astype(BF)
-                part[(*hidx(h), slice(None), pl.ds(latent, 128))] = rotate(v[:, nope:nope + 128])
+                part[(*hidx(h), slice(None), pl.ds(latent, LN))] = rotate(v[:, nope:nope + LN])
 
     q_heads(0, 0, 6)
     g_copy(0).start()
@@ -226,7 +229,7 @@
     r = lax.dot_general(x_ref[:, :ff], gbuf[5, pl.ds(0, lat_row), :], nt, preferred_element_type=F32) + lax.dot_general(x_ref[:, ff:], gbuf[5, pl.ds(lat_row, lat_row), pl.ds(0, OB)], nt, preferred_element_type=F32)
     g_copy(5).start()
     r_lat = r[:, :latent].astype(BF)
-    r_rope = rotate(jnp.concatenate([r[:, latent:], jnp.zeros((num_seq, 128 - rope), F32)], axis=1)).astype(BF)
+    r_rope = rotate(jnp.concatenate([r[:, latent:], jnp.zeros((num_seq, LN - rope), F32)], axis=1)).astype(BF)
     kvf[:, :latent] = r_lat.astype(F32)
     kvf[:, latent:] = r_rope.astype(F32)
     kv_ref[:, :latent] = r_lat
@@ -239,15 +242,15 @@
         for b in range(8):
             c_copy(b, g * 8 + b, 2 * g + b // 4).wait()
         rows8 = pl.ds(pl.multiple_of(g * 8, 8), 8)
-        q = part[:, :, :, rows8, pl.ds(0, latent + 128)].reshape(128, latent + 128).astype(BF)
-        kv_rep = jnp.broadcast_to(kvf[rows8, :][None], (16, 8, latent + 128)).reshape(128, latent + 128)
-        n_rep = jnp.broadcast_to(lenb[rows8, :][None], (16, 8, 128)).reshape(128, 128)
+        q = part[:, :, :, rows8, pl.ds(0, latent + LN)].reshape(LN, latent + LN).astype(BF)
+        kv_rep = jnp.broadcast_to(kvf[rows8, :][None], (16, 8, latent + LN)).reshape(LN, latent + LN)
+        n_rep = jnp.broadcast_to(lenb[rows8, :][None], (16, 8, LN)).reshape(LN, LN)
         n_rep = jnp.concatenate([n_rep, n_rep], axis=1)
-        row = lax.broadcasted_iota(jnp.int32, (128, 256), 0) % 8
-        pos = lax.broadcasted_iota(jnp.int32, (128, 256), 1).astype(F32)
+        row = lax.broadcasted_iota(jnp.int32, (LN, 256), 0) % 8
+        pos = lax.broadcasted_iota(jnp.int32, (LN, 256), 1).astype(F32)
         s_new = jnp.sum(q.astype(F32) * kv_rep, axis=1, keepdims=True) * scale
         q = q[:, :latent + rope]
-        s = jnp.zeros((128, 256), F32)
+        s = jnp.zeros((LN, 256), F32)
         for b in range(8):
             s = jnp.where(row == b, jnp.dot(q, dbuf[cache_at(b, 2 * g + b // 4)], preferred_element_type=F32), s)
         s = jnp.where(pos < n_rep, s * scale, -jnp.inf)
@@ -259,7 +262,7 @@
         o = (e_new / den).astype(BF).astype(F32) * kv_rep[:, :latent]
         for b in range(8):
             o = o + lax.dot_general(jnp.where(row == b, p, 0.0).astype(BF), dbuf[cache_at(b, 2 * g + b // 4)][:latent], nt, preferred_element_type=F32)
-        part[:, :, :, rows8, pl.ds(1024, latent)] = o.reshape(2, 2, 4, 8, latent)
+        part[:, :, :, rows8, pl.ds(1024, latent)] = o.reshape(*ZYC, 8, latent)
 
     for p in range(ND):
         d_copy(p).start()
@@ -270,7 +273,7 @@
     a_copy(3).wait()
     for h in range(num_heads):
         ob = part[(*hidx(h), slice(None), pl.ds(1024, latent))].astype(BF)
-        vcat[:, h * 128:(h + 1) * 128] = jnp.dot(ob, gbuf[3, pl.ds(h % 4 * latent, latent), pl.ds(OB + 128 * (h // 4), 128)], preferred_element_type=F32).astype(BF)
+        vcat[:, h * LN:(h + 1) * LN] = jnp.dot(ob, gbuf[3, pl.ds(h % 4 * latent, latent), pl.ds(OB + LN * (h // 4), LN)], preferred_element_type=F32).astype(BF)
     a_copy(4).wait()
     fwd_zc(None)
     for lo, hi, slot in ((0, ff, 4), (ff, hidden, 3)):
@@ -311,10 +314,10 @@
 
     ntok = 16 * num_seq
     rows = 16 * 8
-    meta = meta_all[...].reshape(ntok, 128)
+    meta = meta_all[...].reshape(ntok, LN)
     meta_t[...] = meta.T
-    lane = lax.broadcasted_iota(jnp.int32, (ntok, 128), 1)
-    base_col = lax.broadcasted_iota(jnp.int32, (ntok, 128), 0) // num_seq * 8
+    lane = lax.broadcasted_iota(jnp.int32, (ntok, LN), 1)
+    base_col = lax.broadcasted_iota(jnp.int32, (ntok, LN), 0) // num_seq * 8
     base_row = lax.broadcasted_iota(jnp.int32, (1, ntok), 1) // num_seq * 8
     slot_row = lax.broadcasted_iota(jnp.int32, (rows, ntok), 0)
     for e in range(num_loc):
@@ -322,7 +325,7 @@
         code = jnp.sum(jnp.where(lane == ge, meta, 0.0), axis=1, keepdims=True)
         gate = jnp.sum(jnp.where(lane == ge + 64, meta, 0.0), axis=1, keepdims=True)
         sel[e] = jnp.where(lane == code.astype(jnp.int32) + base_col, 1.0, 0.0).astype(BF)
-        gates[e] = jnp.broadcast_to(gate, (ntok, 128))
+        gates[e] = jnp.broadcast_to(gate, (ntok, LN))
         code_t = meta_t[pl.ds(ge, 1), :].astype(jnp.int32) + base_row
         sel_t[pl.ds(e * rows, rows), :] = jnp.where(slot_row == code_t, 1.0, 0.0).astype(BF)
 
@@ -396,11 +399,44 @@
         part[c, y, zb, :, cols] = part[c, y, zb, :, cols] + rz[0, :, cols]
         s4(j).start()
 
+    def t3(j, i):
+        return rdma(part.at[c, :, (zc, za)[i], :, chunk(j)], ry.at[pl.ds(2 * i, 2), :, chunk(j)], s3_send.at[2 * j + i], s3_recv.at[2 * j + i], za_peer)
+
+    def t4(j):
+        return rdma(part.at[c, :, zb, :, chunk(j)], rz.at[pl.ds(0, 2), :, chunk(j)], s4_send.at[j], s4_recv.at[j], zb_peer)
+
+    def t2(j):
+        return rdma(part.at[c, 1 - y, z, :, chunk(j)], rz.at[2, :, chunk(j)], s2_send.at[j], s2_recv.at[j], y_peer)
+
+    def turn_a(j):
+        cols = chunk(j)
+        s1(j).wait_recv()
+        part[c, :, :, :, cols] = part[c, :, :, :, cols] + rc[:, :, :, cols]
+        t3(j, 0).start()
+        t3(j, 1).start()
+
+    def turn_b(j):
+        cols = chunk(j)
+        t3(j, 0).wait_recv()
+        part[c, :, zb, :, cols] = part[c, :, zb, :, cols] + ry[0:2, :, cols]
+        t4(j).start()
+
+    def turn_c(j):
+        cols = chunk(j)
+        t3(j, 1).wait_recv()
+        t4(j).wait_recv()
+        part[c, :, z, :, cols] = part[c, :, z, :, cols] + ry[2:4, :, cols] + rz[0:2, :, cols]
+        t2(j).start()
+
     def step_f(j):
         cols = chunk(j)
-        s3(j, 1).wait_recv()
-        s4(j).wait_recv()
-        routed = part[c, y, z, :, cols] + rz[1, :, cols] + rz[2, :, cols]
+        if j in YLAST:
+            t2(j).wait_recv()
+            routed = part[c, y, z, :, cols] + rz[2, :, cols]
+        else:
+            s3(j, 1).wait_recv()
+            s4(j).wait_recv()
+            routed = part[c, y, z, :, cols] + rz[1, :, cols] + rz[2, :, cols]
         out_ref[:, cols] = (h_own[:, cols].astype(F32) + shared[:, cols].astype(F32) + routed).astype(BF)
 
     def down(j):
@@ -413,7 +449,7 @@
             o = jnp.dot(act[e], buf[at[0], at[1], pl.ds(j % 2 * cw + (j // 2 > 1) * (e % 2) * dw, cw)] if buf is gbuf else buf[at[0], :, pl.ds(j % 2 * cw, cw)], preferred_element_type=F32).astype(BF)
             b = jnp.dot(sel[e], o, preferred_element_type=F32)
             gt = gates[e]
-            b = (b * jnp.concatenate([gt] * (cw // 128), axis=1)).reshape(2, 2, 4, num_seq, cw)
+            b = (b * jnp.concatenate([gt] * (cw // LN), axis=1)).reshape(*ZYC, num_seq, cw)
             if e == 0:
                 part[:, :, :, :, cols] = b
             else:
@@ -441,34 +477,57 @@
         o = jnp.dot(act_sh[0], dbuf[2 * i], preferred_element_type=F32) + jnp.dot(act_sh[1], dbuf[2 * i + 1], preferred_element_type=F32)
         shared[:, i * dw:(i + 1) * dw] = o.astype(BF)
 
+    fill = [lambda i=i: shared_up(i) for i in range(6)] + [lambda i=i: shared_down(i) for i in range(4)]
+
+    def work(n):
+        for _ in range(n):
+            fill.pop(0)()
+
+    def enter(j):
+        (turn_a if j in YLAST else step_a)(j)
+
     for j in range(NCH):
         down(j)
         s1(j).start()
         if j >= 1:
-            step_a(j - 1)
+            enter(j - 1)
+        if j == 5:
+            turn_b(0)
         if j == 6:
-            step_b(0)
-    step_a(NCH - 1)
-    fill = [lambda i=i: shared_up(i) for i in range(6)] + [lambda i=i: shared_down(i) for i in range(4)]
-    plan = [1, 2, 2, 2, 1, 1, 1]
-    for j in range(1, NCH):
-        step_b(j)
-        for _ in range(plan[j - 1]):
-            fill.pop(0)()
-        step_c(j - 1)
-        if j == NCH - 1:
-            for i in range(NCH - 1):
-                step_f(i)
-    step_c(NCH - 1)
-    step_f(NCH - 1)
+            step_b(1)
+    enter(7)
+    turn_b(2)
+    step_b(3)
+    step_c(1)
+    work(1)
+    turn_c(0)
+    step_b(4)
+    step_c(3)
+    work(1)
+    step_b(5)
+    step_c(4)
+    work(1)
+    turn_c(2)
+    step_b(6)
+    step_c(5)
+    work(1)
+    step_b(7)
+    step_c(6)
+    work(3)
+    step_c(7)
+    work(3)
+    for j in range(NCH):
+        step_f(j)
     for a in started:
         a.wait_send()
     for j in range(NCH):
         s1(j).wait_send()
-        s2(j).wait_send()
-        s3(j, 0).wait_send()
-        s3(j, 1).wait_send()
-        s4(j).wait_send()
+        if j in YLAST:
+            copies = (t2(j), t3(j, 0), t3(j, 1), t4(j))
+        else:
+            copies = (s2(j), s3(j, 0), s3(j, 1), s4(j))
+        for a in copies:
+            a.wait_send()
 
 
 def layer(x, lens, routes, route_gates, cache, w_q, w_dkv, w_uk, w_uv, w_o, sh_gate, sh_up, sh_down, ex_gate, ex_up, ex_down):
@@ -487,23 +546,23 @@
         scratch_shapes=[
             pltpu.VMEM((NG, hidden, ff), BF),
             pltpu.VMEM((ND, ff, 2 * hidden // NCH), BF),
-            pltpu.VMEM((16, num_seq, 128), BF),
+            pltpu.VMEM((16, num_seq, LN), BF),
             pltpu.VMEM((num_seq, 640), F32),
-            pltpu.VMEM((num_seq, 128), F32),
+            pltpu.VMEM((num_seq, LN), F32),
             pltpu.VMEM((num_seq, hidden), BF),
             pltpu.VMEM((num_seq, hidden), BF),
-            pltpu.VMEM((num_seq, 128), F32),
-            pltpu.VMEM((2, 2, 4, num_seq, hidden), BF),
-            pltpu.VMEM((2, 2, 4, num_seq, 128), F32),
-            pltpu.VMEM((128, ntok), F32),
-            pltpu.VMEM((num_loc, ntok, 128), BF),
-            pltpu.VMEM((num_loc * 128, ntok), BF),
-            pltpu.VMEM((num_loc, ntok, 128), F32),
-            pltpu.VMEM((num_loc * 128, hidden), BF),
-            pltpu.VMEM((num_loc, 128, ff), BF),
+            pltpu.VMEM((num_seq, LN), F32),
+            pltpu.VMEM((*ZYC, num_seq, hidden), BF),
+            pltpu.VMEM((*ZYC, num_seq, LN), F32),
+            pltpu.VMEM((LN, ntok), F32),
+            pltpu.VMEM((num_loc, ntok, LN), BF),
+            pltpu.VMEM((num_loc * LN, ntok), BF),
+            pltpu.VMEM((num_loc, ntok, LN), F32),
+            pltpu.VMEM((num_loc * LN, hidden), BF),
+            pltpu.VMEM((num_loc, LN, ff), BF),
             pltpu.VMEM((2, num_seq, ff), BF),
             pltpu.VMEM((num_seq, hidden), BF),
-            pltpu.VMEM((2, 2, 4, num_seq, hidden), F32),
+            pltpu.VMEM((*ZYC, num_seq, hidden), F32),
             pltpu.VMEM((2, 4, num_seq, hidden), F32),
             pltpu.VMEM((4, num_seq, hidden), F32),
             pltpu.VMEM((3, num_seq, hidden), F32),
@@ -515,12 +574,22 @@
     )(x, lens, routes, route_gates, cache, w_q, w_dkv, w_uk, w_uv, w_o, sh_gate, sh_up, sh_down, ex_gate, ex_up, ex_down)
 
 
+def finish_kernel(a_ref, b_ref, c_ref, d_ref):
+    c_ref[...] = a_ref[...]
+    d_ref[...] = b_ref[...]
+
+
+def finish(a, b):
+    vm = pl.BlockSpec(memory_space=pltpu.VMEM)
+    return pl.pallas_call(finish_kernel, out_shape=(jax.ShapeDtypeStruct(a.shape, a.dtype), jax.ShapeDtypeStruct(b.shape, b.dtype)), in_specs=[vm, vm], out_specs=(vm, vm), name="finish")(a, b)
+
+
 def solution(mesh):
     def device_step(x_blk, cache_blk, len_blk, routes, route_gates, w_q, w_dkv, w_uk, w_uv, w_o, sh_gate, sh_up, sh_down, ex_gate, ex_up, ex_down):
         lens = len_blk[None, :]
         uk = w_uk.reshape(-1, w_uk.shape[2])
         uv = w_uv.reshape(-1, w_uv.shape[2])
-        return layer(x_blk, lens, routes.T, route_gates.T, cache_blk.transpose(0, 2, 1), w_q, w_dkv.T, uk, uv, w_o, sh_gate, sh_up, sh_down, ex_gate, ex_up, ex_down)
+        return finish(*layer(x_blk, lens, routes.T, route_gates.T, cache_blk.transpose(0, 2, 1), w_q, w_dkv.T, uk, uv, w_o, sh_gate, sh_up, sh_down, ex_gate, ex_up, ex_down))
 
     batch_spec = P(("dp", "ep"))
     weight_spec = P()

time: 93 us -> 87.9 us (0.945)
  local copies, waits for them, and re-layouts: 2.97 us -> 0 us
  Pallas kernels: 89.2 us -> 87.1 us
    pallas_call x1, Pallas kernels: 89.2 us -> 85.5 us  [layer(): pl.pallas_call(layer_kernel, out_shape=(jax.ShapeDtypeStruct((num_seq, hi...]
    unnamed x2 -> x0, local copies, waits for them, and re-layouts: 2.97 us -> none
    pallas_call x0 -> x1, Pallas kernels: none -> 1.58 us  [finish(): pl.pallas_call(finish_kernel, out_shape=(jax.ShapeDtypeStruct(a.shape, a....]
where the time goes in v7:
time: 87.9 us; the launch traced here: 87.7 us
  Pallas kernels  87.1 us (99%)
    pallas_call x1, Pallas kernels, layer(): pl.pallas_call(layer_kernel, out_shape=(jax.ShapeDtypeStruct((num_seq, hi...  85.5 us

profile of v7, /device:TPU:0, one launch (start us, length us, event | category | flops | bytes accessed | tf_op | source)
XLA Modules:
  0.0 87.7 jit_solution(4357617128898784027)
XLA Ops:
  0.6 85.5 %layer.1 = (bf16[32,2048]{1,0:T(8,128)(2,1)}, bf16[32,576]{1,0:T(8,128)(2,1)}) custom-call(bf16[32,2048]{1,0:T(8,128)(2,1)} %x_ref.1, s32[1,32]{1,0:T(1,128)} %bitcast.13, s32[6,32]{1,0:T(8,128)} %bitcast.11, f32[6,32]{1,0:T(8,128)} %bitcast.12, bf16[32,576,256]{2,1,0:T(8,128)(2,1)} %bitcast.7, bf16[2048,3072]{1,0:T(8,128)(2,1)} %wq_ref.1, ...), custom_call_target="tpu_custom_call" | custom-call | tf_op jit(solution)/shard_map/layer/pallas_call | solution.py:541
  86.1 1.6 %finish.1 = (bf16[32,2048]{1,0:T(8,128)(2,1)}, bf16[32,576]{1,0:T(8,128)(2,1)}) custom-call(bf16[32,2048]{1,0:T(8,128)(2,1)} %get-tuple-element.4.a_ref, bf16[32,576]{1,0:T(8,128)(2,1)} %get-tuple-element.5.b_ref), custom_call_target="tpu_custom_call" | custom-call | tf_op jit(solution)/shard_map/finish/pallas_call | solution.py:584

commit v8 on v7

--- a/solution.py
+++ b/solution.py
@@ -18,7 +18,7 @@
 NCH = 8
 NA = 2
 ZYC = (2, 2, 4)
-YLAST = (0, 2)
+YLAST = (0, 1)
 
 
 def layer_kernel(x_ref, len_ref, routes_ref, rgate_ref, cache_ref, wq_ref, wdkv_ref, wuk_ref, wuv_ref, wo_ref,
@@ -491,23 +491,24 @@
         s1(j).start()
         if j >= 1:
             enter(j - 1)
-        if j == 5:
+        if j == 4:
             turn_b(0)
         if j == 6:
-            step_b(1)
+            turn_b(1)
+        if j == 7:
+            step_b(2)
     enter(7)
-    turn_b(2)
     step_b(3)
-    step_c(1)
+    step_c(2)
     work(1)
     turn_c(0)
     step_b(4)
     step_c(3)
     work(1)
+    turn_c(1)
     step_b(5)
     step_c(4)
     work(1)
-    turn_c(2)
     step_b(6)
     step_c(5)
     work(1)

time: 87.9 us -> 86.7 us (0.986)
  Pallas kernels: 87.1 us -> 85.9 us
    pallas_call x1, Pallas kernels: 85.5 us -> 84.3 us  [layer(): pl.pallas_call(layer_kernel, out_shape=(jax.ShapeDtypeStruct((num_seq, hi...]
where the time goes in v8:
time: 86.7 us; the launch traced here: 86.5 us
  Pallas kernels  85.9 us (99%)
    pallas_call x1, Pallas kernels, layer(): pl.pallas_call(layer_kernel, out_shape=(jax.ShapeDtypeStruct((num_seq, hi...  84.3 us

profile of v8, /device:TPU:0, one launch (start us, length us, event | category | flops | bytes accessed | tf_op | source)
XLA Modules:
  0.0 86.5 jit_solution(3437861905651352337)
XLA Ops:
  0.6 84.3 %layer.1 = (bf16[32,2048]{1,0:T(8,128)(2,1)}, bf16[32,576]{1,0:T(8,128)(2,1)}) custom-call(bf16[32,2048]{1,0:T(8,128)(2,1)} %x_ref.1, s32[1,32]{1,0:T(1,128)} %bitcast.13, s32[6,32]{1,0:T(8,128)} %bitcast.11, f32[6,32]{1,0:T(8,128)} %bitcast.12, bf16[32,576,256]{2,1,0:T(8,128)(2,1)} %bitcast.7, bf16[2048,3072]{1,0:T(8,128)(2,1)} %wq_ref.1, ...), custom_call_target="tpu_custom_call" | custom-call | tf_op jit(solution)/shard_map/layer/pallas_call | solution.py:542
  85.0 1.6 %finish.1 = (bf16[32,2048]{1,0:T(8,128)(2,1)}, bf16[32,576]{1,0:T(8,128)(2,1)}) custom-call(bf16[32,2048]{1,0:T(8,128)(2,1)} %get-tuple-element.4.a_ref, bf16[32,576]{1,0:T(8,128)(2,1)} %get-tuple-element.5.b_ref), custom_call_target="tpu_custom_call" | custom-call | tf_op jit(solution)/shard_map/finish/pallas_call | solution.py:585
